TPU v7x, 32 devices: a whole 2x2x4 slice. The times are simulated.
32 devices in a mesh: ia: 4 (over y, x), ja: 4 (over z), col: 2 (over core).
Axes of the slice: x: 2, y: 2, z: 4, core: 2. Of those that a mesh axis runs over, the one named last changes fastest.
Arguments:
- pair_rep: bfloat16 [512, 512, 128], P('ia', 'ja'), may hold values from -6 to 6
- norm_gain: float32 [128], replicated, may hold values from 0.1 to 1.9
- weights: bfloat16 [4, 128, 128], P(None, None, 'col'), may hold values from -0.5 to 0.5
- residue_mask: int32 [512], replicated, may hold values 0 or 1
- product_grad: bfloat16 [512, 128, 512], P('ia', 'col', 'ja'), may hold values from -1 to 1
Outputs:
- pair_grad: bfloat16 [512, 512, 128], P('ia', 'ja')
- weight_grads: float32 [4, 128, 128], P(None, None, 'col')
All inputs are finite; a program needn't handle non-finite values.
Results may differ from a plain program's by a relative error of at most 0.0067.
Values may be sent and summed in bfloat16 or wider, within the bound.
A program may use at most 128 MiB of HBM per device.

v0:
```python
import functools
import math

import jax
import jax.numpy as jnp
from jax import lax
from jax.experimental import pallas as pl
from jax.experimental.pallas import tpu as pltpu
from jax.sharding import PartitionSpec as P

CLIP_LIMIT = 64.0
MAX_CHUNKS = 4
MESH = pl.DeviceIdType.MESH
NT = (((1,), (1,)), ((), ()))
NN = (((1,), (0,)), ((), ()))
F32 = jnp.float32
BF16 = jnp.bfloat16


def partner(index, step, count):
    if count & (count - 1) == 0:
        return index ^ step
    return (step - index + count) % count


def exchange(value, axis, step, count):
    return lax.ppermute(value, axis, [(a, partner(a, step, count)) for a in range(count)])


def dot(a, b, dims):
    return lax.dot_general(a, b, dims, preferred_element_type=F32)


def eye(n):
    rows = lax.broadcasted_iota(jnp.int32, (n, n), 0)
    cols = lax.broadcasted_iota(jnp.int32, (n, n), 1)
    return jnp.where(rows == cols, 1.0, 0.0).astype(BF16)


class Sizes:
    def __init__(self, na, nz, nh, rows, cols, depth, ch):
        self.na, self.nz, self.nh = na, nz, nh
        self.rb, self.k, self.d, self.ch = rows, cols, depth, ch
        self.g = na * nh
        self.rh = rows // nh
        self.hid = ch * nh
        self.cp = ch // na
        self.nq = math.gcd(self.cp, MAX_CHUNKS)
        self.cq = self.cp // self.nq
        self.nc = self.g * self.cq
        self.i = na * rows
        self.br = math.gcd(self.rh, 16)
        self.nb = self.rh // self.br
        self.sp = self.hid + 8
        self.tp = self.br + 8


def kernel(z_, p_ref, x_hbm, wall_ref, wt_ref, gain_ref, pv_ref, out_ref, raw_ref,
           xv, pg, unit_s, inv_s, nt_s, pr, fac, relay, lrs, lrb, gs, gr, turn, ng,
           xsem, psend, precv, zsend, zrecv, lsend, lrecv, gsend, grecv, osend, orecv):
    s = z_
    na, nz, nh, g_n, nq, cq, cp, nc = s.na, s.nz, s.nh, s.g, s.nq, s.cq, s.cp, s.nc
    rb, rh, k, d, hid, br, nb = s.rb, s.rh, s.k, s.d, s.hid, s.br, s.nb
    a, z, h = lax.axis_index("ia"), lax.axis_index("ja"), lax.axis_index("col")
    me_g = h * na + a
    row0 = a * rb + h * rh

    def plane(g):
        return (lax.rem(g, na), z, lax.div(g, na))

    def peer_g(step):
        return lax.rem(me_g + step, g_n)

    def from_g(step):
        return lax.rem(me_g + g_n - step, g_n)

    barrier = pltpu.get_barrier_semaphore()
    for step in range(1, g_n):
        pl.semaphore_signal(barrier, inc=1, device_id=plane(peer_g(step)), device_id_type=MESH)

    @pl.when(z > 0)
    def _():
        pl.semaphore_signal(barrier, inc=1, device_id=(a, z - 1, h), device_id_type=MESH)

    @pl.when(z < nz - 1)
    def _():
        pl.semaphore_signal(barrier, inc=1, device_id=(a, z + 1, h), device_id_type=MESH)

    xcopy = pltpu.make_async_copy(x_hbm.at[pl.ds(h * rh, rh)], xv, xsem)
    xcopy.start()
    ends = jnp.where(z > 0, 1, 0) + jnp.where(z < nz - 1, 1, 0)
    pl.semaphore_wait(barrier, g_n - 1 + ends)

    def p_copy(q, step):
        return pltpu.make_async_remote_copy(
            src_ref=p_ref.at[lax.rem(a + step, na), q],
            dst_ref=pg.at[z, pl.ds(q * cq, cq), pl.ds(a * rb, rb)],
            send_sem=psend.at[q, step], recv_sem=precv.at[q, step],
            device_id=(lax.rem(a + step, na), z, h), device_id_type=MESH)

    for q in range(nq):
        for step in range(1, na):
            p_copy(q, step).start()
    for q in range(nq):
        for r in range(cq):
            pg[z, q * cq + r, pl.ds(a * rb, rb), :] = p_ref[a, q, r]

    def z_copy(q, block, up):
        ref = pg.at[block, pl.ds(q * cq, cq)]
        return pltpu.make_async_remote_copy(
            src_ref=ref, dst_ref=ref,
            send_sem=zsend.at[q, block, 0 if up else 1], recv_sem=zrecv.at[q, block],
            device_id=(a, z + 1 if up else z - 1, h), device_id_type=MESH)

    def z_own(q):
        for step in range(1, na):
            p_copy(q, step).wait_recv()

        @pl.when(z < nz - 1)
        def _():
            z_copy(q, z, True).start()

        @pl.when(z > 0)
        def _():
            z_copy(q, z, False).start()

    def z_hop(q, hop):
        @pl.when(z >= hop)
        def _():
            z_copy(q, z - hop, True).wait_recv()

            @pl.when(z < nz - 1)
            def _():
                z_copy(q, z - hop, True).start()

        @pl.when(z + hop < nz)
        def _():
            z_copy(q, z + hop, False).wait_recv()

            @pl.when(z > 0)
            def _():
                z_copy(q, z + hop, False).start()

    eye_d = eye(d)
    xcopy.wait()

    def rows_step(t, sub):
        x2 = xv[pl.ds(2 * t, 2)].reshape(2 * k, d)
        xt = dot(eye_d, x2, NT)
        centred = xt - jnp.mean(xt, axis=0, keepdims=True)
        inv = lax.rsqrt(jnp.mean(centred * centred, axis=0, keepdims=True) + 1e-05)
        unit = centred * inv
        normed = (unit * gain_ref[...]).astype(BF16)
        unit_s[t] = unit
        inv_s[t] = inv
        nt_s[t] = normed
        pr[...] = dot(wall_ref[...], normed, NN)
        valid = pv_ref[pl.ds(h * (rh // 2) + t, 1), :]
        for q in range(nq):
            for side in range(2):
                lin = pr[pl.ds((2 * side) * hid + q * nc, nc), :]
                gate = jax.nn.sigmoid(pr[pl.ds((2 * side + 1) * hid + q * nc, nc), :])
                first = valid * gate
                value = first * lin
                fac[t, q, 2 * side] = first.astype(BF16)
                fac[t, q, 2 * side + 1] = (value * (1.0 - gate)).astype(BF16)
                for e in range(2):
                    at = pl.multiple_of((2 * sub + e) * s.sp, 8) + q * nc
                    relay[side, pl.ds(at, nc), :] = value[:, e * k:(e + 1) * k]

    for b in range(nb):
        def one(sub, carry, b=b):
            rows_step(b * (br // 2) + sub, sub)
            return carry
        lax.fori_loop(0, br // 2, one, 0)

        def flush(c, carry, b=b):
            for side in range(2):
                tile = relay[side, pl.ds(c, br, stride=s.sp), :]
                lrs[side, c, pl.ds(b * br, br), :] = tile.astype(BF16)
            return carry
        lax.fori_loop(0, hid, flush, 0, unroll=4)
        if b < nq:
            z_own(b)
    for q in range(nb, nq):
        z_own(q)

    def lr_copy(q, step):
        return pltpu.make_async_remote_copy(
            src_ref=lrs.at[:, pl.ds(q * nc + peer_g(step) * cq, cq)],
            dst_ref=lrb.at[:, pl.ds(q * cq, cq), pl.ds(row0, rh)],
            send_sem=lsend.at[q, step], recv_sem=lrecv.at[q, step],
            device_id=plane(peer_g(step)), device_id_type=MESH)

    for q in range(nq):
        for step in range(1, g_n):
            lr_copy(q, step).start()
    for q in range(nq):
        for side in range(2):
            for r in range(cq):
                lrb[side, q * cq + r, pl.ds(row0, rh), :] = lrs[side, q * nc + me_g * cq + r]

    eye_k = eye(k)

    def triangle(c):
        panel = jnp.concatenate([pg[b, c] for b in range(nz)], axis=1)
        left, right = lrb[0, c], lrb[1, c]
        gs[0, c] = dot(panel, right, NN).astype(BF16)
        left_t = dot(eye_k, left, NT).astype(BF16)
        back_t = dot(left_t, panel, NN).astype(BF16)
        for b in range(nz):
            gs[1, c, b * k:(b + 1) * k, :] = dot(eye_k, back_t[:, b * k:(b + 1) * k], NT).astype(BF16)

    def g_copy(q, step):
        g = peer_g(step)
        return pltpu.make_async_remote_copy(
            src_ref=gs.at[:, pl.ds(q * cq, cq), pl.ds(lax.rem(g, na) * rb + lax.div(g, na) * rh, rh)],
            dst_ref=gr.at[:, pl.ds(q * nc + me_g * cq, cq)],
            send_sem=gsend.at[q, step], recv_sem=grecv.at[q, step],
            device_id=plane(g), device_id_type=MESH)

    def out_copy(b, step):
        ref = out_ref.at[pl.ds(h * rh + b * br, br)]
        return pltpu.make_async_remote_copy(
            src_ref=ref, dst_ref=ref, send_sem=osend.at[b, step], recv_sem=orecv.at[b, step],
            device_id=(a, z, lax.rem(h + step, nh)), device_id_type=MESH)

    def collect(q):
        for step in range(1, g_n):
            g_copy(q, step).wait_recv()
        raw_ref[q] = jnp.zeros((4 * nc, d), F32)
        for b in range(nb):
            def spread(n, carry, b=b):
                for side in range(2):
                    tile = gr[side, q * nc + n, pl.ds(b * br, br), :].astype(F32)
                    turn[side, pl.ds(pl.multiple_of(n * s.tp, 8), br), :] = tile
                return carry
            lax.fori_loop(0, nc, spread, 0, unroll=4)

            def one(sub, carry, b=b):
                t = b * (br // 2) + sub
                parts = []
                for side in range(2):
                    both = jnp.concatenate(
                        [turn[side, pl.ds(2 * sub + e, nc, stride=s.tp), :] for e in range(2)], axis=1)
                    for w in range(2):
                        parts.append((both * fac[t, q, 2 * side + w].astype(F32)).astype(BF16))
                grads = jnp.concatenate(parts, axis=0)
                raw_ref[q] += dot(grads, nt_s[t], NT)
                part = dot(wt_ref[q], grads, NN)
                if q:
                    part = part + ng[t]
                if q < nq - 1:
                    ng[t] = part
                else:
                    unit = unit_s[t]
                    scaled = part * gain_ref[...]
                    first = jnp.mean(scaled, axis=0, keepdims=True)
                    second = jnp.mean(scaled * unit, axis=0, keepdims=True)
                    res = (inv_s[t] * (scaled - first - unit * second)).astype(BF16)
                    for e in range(2):
                        out_ref[h * rh + 2 * t + e] = dot(
                            eye_k, res[:, e * k:(e + 1) * k], NT).astype(BF16)
                return carry
            lax.fori_loop(0, br // 2, one, 0)
            if q == nq - 1:
                for step in range(1, nh):
                    out_copy(b, step).start()

    for hop in range(1, nz - 1):
        for q in range(nq):
            z_hop(q, hop)
    for q in range(nq):
        z_hop(q, nz - 1)
        for step in range(1, g_n):
            lr_copy(q, step).wait_recv()

        def tri(r, carry, q=q):
            triangle(q * cq + r)
            return carry
        lax.fori_loop(0, cq, tri, 0)
        for step in range(1, g_n):
            g_copy(q, step).start()
        for side in range(2):
            for r in range(cq):
                gr[side, q * nc + me_g * cq + r] = gs[side, q * cq + r, pl.ds(row0, rh), :]
        if q:
            collect(q - 1)
    collect(nq - 1)

    for b in range(nb):
        for step in range(1, nh):
            out_copy(b, step).wait()
    for q in range(nq):
        for step in range(1, na):
            p_copy(q, step).wait_send()
        for step in range(1, g_n):
            lr_copy(q, step).wait_send()
            g_copy(q, step).wait_send()
        for hop in range(nz):
            @pl.when((z >= hop) & (z < nz - 1))
            def _(q=q, hop=hop):
                z_copy(q, z - hop, True).wait_send()

            @pl.when((z + hop < nz) & (z > 0))
            def _(q=q, hop=hop):
                z_copy(q, z + hop, False).wait_send()


def on_device(na, nz, nh, pair_rep, norm_gain, weights, residue_mask, product_grad):
    rows, cols, depth = pair_rep.shape
    ch = product_grad.shape[1]
    s = Sizes(na, nz, nh, rows, cols, depth, ch)
    panels = product_grad.transpose(1, 0, 2).reshape(na, s.nq, s.cq, rows, cols)
    every = lax.all_gather(weights, "col", axis=0)
    every = every.reshape(nh, 4, depth, na, s.nq, s.cq)
    wall = every.transpose(1, 4, 0, 3, 5, 2).reshape(4 * s.hid, depth)
    wt = every.transpose(4, 2, 1, 0, 3, 5).reshape(s.nq, depth, 4 * s.nc)
    gain = jnp.broadcast_to(norm_gain[:, None], (depth, 2 * cols))
    validity = residue_mask.astype(F32)
    row_valid = lax.dynamic_slice_in_dim(validity, lax.axis_index("ia") * rows, rows)
    col_valid = lax.dynamic_slice_in_dim(validity, lax.axis_index("ja") * cols, cols)
    valid = (row_valid[:, None] * col_valid[None, :]).reshape(rows // 2, 2 * cols)

    vm = pl.BlockSpec(memory_space=pltpu.VMEM)
    dma = pltpu.SemaphoreType.DMA
    half = s.rh // 2
    scratch = [
        pltpu.VMEM((s.rh, cols, depth), BF16),
        pltpu.VMEM((nz, s.cp, s.i, cols), BF16),
        pltpu.VMEM((half, depth, 2 * cols), F32),
        pltpu.VMEM((half, 1, 2 * cols), F32),
        pltpu.VMEM((half, depth, 2 * cols), BF16),
        pltpu.VMEM((4 * s.hid, 2 * cols), F32),
        pltpu.VMEM((half, s.nq, 4, s.nc, 2 * cols), BF16),
        pltpu.VMEM((2, s.br * s.sp, cols), F32),
        pltpu.VMEM((2, s.hid, s.rh, cols), BF16),
        pltpu.VMEM((2, s.cp, s.i, cols), BF16),
        pltpu.VMEM((2, s.cp, s.i, cols), BF16),
        pltpu.VMEM((2, s.hid, s.rh, cols), BF16),
        pltpu.VMEM((2, s.nc * s.tp, cols), F32),
        pltpu.VMEM((half, depth, 2 * cols), F32),
        dma(()), dma((s.nq, na)), dma((s.nq, na)), dma((s.nq, nz, 2)), dma((s.nq, nz)),
        dma((s.nq, s.g)), dma((s.nq, s.g)), dma((s.nq, s.g)), dma((s.nq, s.g)),
        dma((s.nb, nh)), dma((s.nb, nh)),
    ]
    pair_grad, raw = pl.pallas_call(
        functools.partial(kernel, s),
        out_shape=(
            jax.ShapeDtypeStruct((rows, cols, depth), BF16),
            jax.ShapeDtypeStruct((s.nq, 4 * s.nc, depth), F32),
        ),
        in_specs=[vm, pl.BlockSpec(memory_space=pl.ANY), vm, vm, vm, vm],
        out_specs=(vm, vm),
        scratch_shapes=scratch,
        compiler_params=pltpu.CompilerParams(
            collective_id=0, has_side_effects=True, vmem_limit_bytes=66 * 1000 * 1000),
    )(panels, pair_rep, wall, wt, gain, valid)

    raw = raw.reshape(s.nq, 4, nh, na, s.cq, depth)
    parts = raw.transpose(2, 1, 5, 3, 0, 4).reshape(nh, 4, depth, ch)
    if nh == 2:
        mine = lax.axis_index("col")
        other = lax.dynamic_index_in_dim(parts, 1 - mine, 0, keepdims=False)
        summed = lax.dynamic_index_in_dim(parts, mine, 0, keepdims=False) + exchange(other, "col", 1, 2)
    else:
        summed = lax.dynamic_index_in_dim(lax.psum(parts, "col"), lax.axis_index("col"), 0, keepdims=False)
    for axis, count in (("ia", na), ("ja", nz)):
        if count & (count - 1):
            summed = lax.psum(summed, axis)
            continue
        step = 1
        while step < count:
            summed = summed + exchange(summed, axis, step, count)
            step *= 2
    squares = lax.psum(jnp.sum(summed * summed), "col")
    factor = jnp.minimum(1.0, CLIP_LIMIT * lax.rsqrt(squares + 1e-06))
    return (pair_grad, summed * factor)


def solution(mesh):
    sizes = mesh.shape["ia"], mesh.shape["ja"], mesh.shape["col"]
    placed = (P("ia", "ja", None), P(), P(None, None, "col"), P(), P("ia", "col", "ja"))

    def step(*args):
        return on_device(*sizes, *args)

    return jax.shard_map(
        step,
        mesh=mesh,
        in_specs=placed,
        out_specs=(P("ia", "ja", None), P(None, None, "col")),
        check_vma=False,
    )
```

profile of v0, /device:TPU:0, one launch (start us, length us, event | category | flops | bytes accessed | tf_op | source)
XLA Modules:
  0.0 229.6 jit_solution(10678526980729472778)
XLA Ops:
  0.6 2.2 all-gather
  3.0 0.7 copy.16
  3.7 0.7 convert_element_type.3
  4.3 0.1 fusion
  4.4 0.1 mul.38
  4.6 0.8 copy.18.wt_ref
  5.3 4.3 %copy.15 = bf16[64,128,128]{2,1,0:T(8,128)(2,1)} copy(bf16[64,128,128]{2,0,1:T(8,128)(2,1)} %bitcast.23) | data formatting | bytes 4194304 | tf_op jit(solution)/shard_map/transpose | solution.py:314
  9.6 0.1 mul.39
  9.7 0.6 bitcast_multiply_fusion.pv_ref
  10.4 0.7 broadcast_in_dim.2.gain_ref
  11.1 182.4 %shard_map.68 = (bf16[128,128,128]{2,1,0:T(8,128)(2,1)}, f32[4,128,128]{2,1,0:T(8,128)}) custom-call(bf16[4,4,4,128,128]{4,3,2,1,0:T(8,128)(2,1)} %bitcast.22, bf16[128,128,128]{2,1,0:T(8,128)(2,1)} %x_hbm.1, bf16[512,128]{1,0:T(8,128)(2,1)} %bitcast.28, bf16[4,128,128]{2,1,0:T(8,128)(2,1)} %copy.18.wt_ref, f32[128,256]{1,0:T(8,128)} %broadcast_in_dim.2.gain_ref, ...), custom_call_target="tpu_custom_call" | custom-call | tf_op jit(solution)/shard_map/pallas_call | solution.py:347
  193.5 1.0 copy.19
  194.5 0.4 collective-permute-start
  194.9 1.0 collective-permute-done
  195.9 2.5 %collective-permute-start.1 = (f32[4,128,64]{1,2,0:T(8,128)S(1)}, f32[4,128,64]{1,2,0:T(8,128)S(1)}, u32[]{:S(2)}, u32[]{:S(2)}) collective-permute-start(f32[4,128,64]{1,2,0:T(8,128)S(1)} %bitcast_add_fusion), channel_id=1, source_target_pairs={{0,8},{8,0},{16,24},{24,16},{1,9},{9,1},{17,25},{25,17},{2,10},{10... | collective-permute-start | bytes 393224 | tf_op jit(solution)/shard_map/ppermute | solution.py:27
  198.5 4.0 %collective-permute-done.1 = f32[4,128,64]{1,2,0:T(8,128)S(1)} collective-permute-done((f32[4,128,64]{1,2,0:T(8,128)S(1)}, f32[4,128,64]{1,2,0:T(8,128)S(1)}, u32[]{:S(2)}, u32[]{:S(2)}) %collective-permute-start.1) | collective-permute-done | bytes 131104 | tf_op jit(solution)/shard_map/ppermute | solution.py:27
  202.6 5.2 %collective-permute-done.2 = f32[4,128,64]{1,2,0:T(8,128)S(1)} collective-permute-done((f32[4,128,64]{1,2,0:T(8,128)S(1)}, f32[4,128,64]{1,2,0:T(8,128)S(1)}, u32[]{:S(2)}, u32[]{:S(2)}) %collective-permute-start.2) | collective-permute-done | bytes 131104 | tf_op jit(solution)/shard_map/ppermute | solution.py:27
  207.8 5.0 %collective-permute-done.3 = f32[4,128,64]{1,2,0:T(8,128)S(1)} collective-permute-done((f32[4,128,64]{1,2,0:T(8,128)S(1)}, f32[4,128,64]{1,2,0:T(8,128)S(1)}, u32[]{:S(2)}, u32[]{:S(2)}) %collective-permute-start.3) | collective-permute-done | bytes 131104 | tf_op jit(solution)/shard_map/ppermute | solution.py:27
  212.8 1.1 collective-permute-start.4
  213.9 5.8 %collective-permute-done.4 = f32[4,128,64]{1,2,0:T(8,128)S(1)} collective-permute-done((f32[4,128,64]{1,2,0:T(8,128)S(1)}, f32[4,128,64]{1,2,0:T(8,128)S(1)}, u32[]{:S(2)}, u32[]{:S(2)}) %collective-permute-start.4) | collective-permute-done | bytes 131104 | tf_op jit(solution)/shard_map/ppermute | solution.py:27
  219.7 0.6 multiply_reduce_fusion
  220.3 3.1 %psum.7 = f32[]{:T(128)} all-reduce(f32[]{:T(128)} %get-tuple-element.6), channel_id=1, replica_groups=mesh['ia'=4,'ja'=4,'col'=2] {'col'}, use_global_device_ids=true, to_apply=%region_1.2 | all-reduce | flops 1 | bytes 8 | tf_op jit(solution)/shard_map/psum | solution.py:376
  224.1 0.7 broadcast_multiply_fusion
  224.8 4.8 %copy.23 = bf16[128,128,128]{2,1,0:T(8,128)(2,1)} copy(bf16[128,128,128]{2,1,0:T(8,128)(2,1)} %get-tuple-element.12) | data formatting | bytes 8388608
  (11 shorter events, 0.3 us)
Async XLA Ops:
  0.6 9.7 %copy-start = (f32[128]{0:T(128)S(1)}, f32[128]{0:T(128)}, u32[]{:S(2)}) copy-start(f32[128]{0:T(128)} %param.6) | copy-start | bytes 1540
  194.5 1.4 collective-permute-start
  195.9 6.5 %collective-permute-start.1 = (f32[4,128,64]{1,2,0:T(8,128)S(1)}, f32[4,128,64]{1,2,0:T(8,128)S(1)}, u32[]{:S(2)}, u32[]{:S(2)}) collective-permute-start(f32[4,128,64]{1,2,0:T(8,128)S(1)} %bitcast_add_fusion), channel_id=1, source_target_pairs={{0,8},{8,0},{16,24},{24,16},{1,9},{9,1},{17,25},{25,17},{2,10},{10... | collective-permute-start | bytes 393224 | tf_op jit(solution)/shard_map/ppermute | solution.py:27
  202.5 5.3 %collective-permute-start.2 = (f32[4,128,64]{1,2,0:T(8,128)S(1)}, f32[4,128,64]{1,2,0:T(8,128)S(1)}, u32[]{:S(2)}, u32[]{:S(2)}) collective-permute-start(f32[4,128,64]{1,2,0:T(8,128)S(1)} %add.39), channel_id=1, source_target_pairs={{0,16},{8,24},{16,0},{24,8},{1,17},{9,25},{17,1},{25,9},{2,18},{10... | collective-permute-start | bytes 393224 | tf_op jit(solution)/shard_map/ppermute | solution.py:27
  207.8 5.0 %collective-permute-start.3 = (f32[4,128,64]{1,2,0:T(8,128)S(1)}, f32[4,128,64]{1,2,0:T(8,128)S(1)}, u32[]{:S(2)}, u32[]{:S(2)}) collective-permute-start(f32[4,128,64]{1,2,0:T(8,128)S(1)} %add.40), channel_id=1, source_target_pairs={{0,2},{2,0},{4,6},{6,4},{1,3},{3,1},{5,7},{7,5},{8,10},{10,8},{12,... | collective-permute-start | bytes 393224 | tf_op jit(solution)/shard_map/ppermute | solution.py:27
  212.8 6.9 %collective-permute-start.4 = (f32[4,128,64]{1,2,0:T(8,128)S(1)}, f32[4,128,64]{1,2,0:T(8,128)S(1)}, u32[]{:S(2)}, u32[]{:S(2)}) collective-permute-start(f32[4,128,64]{1,2,0:T(8,128)S(1)} %add.41), channel_id=1, source_target_pairs={{0,4},{2,6},{4,0},{6,2},{1,5},{3,7},{5,1},{7,3},{8,12},{10,14},{12... | collective-permute-start | bytes 393224 | tf_op jit(solution)/shard_map/ppermute | solution.py:27
where the time goes:
time: 230 us
  Pallas kernels  182 us (79%)
  waiting for transfers between devices  20.9 us (9%)
  local copies, waits for them, and re-layouts  12.7 us (6%)
  blocking collectives  5.33 us (2%)
  starting transfers between devices  4.17 us (2%)
  other arithmetic  2.68 us (1%)
    pallas_call x1, Pallas kernels, on_device(): pl.pallas_call(functools.partial(kernel, s), out_shape=(jax.ShapeDtypeStr...  182 us
    ppermute x5, waiting for transfers between devices, exchange(): lax.ppermute(value, axis, [(a, partner(a, step, count)) for a in range(co...  20.9 us
    unnamed x3, local copies, waits for them, and re-layouts  4.79 us
  transfers between devices with their start and end apart: 5, of which 5 were waited for; matrix products, arithmetic and copies ran while one was open for 0% of the time, Pallas kernels for 0%

commit v1 on v0

v1 whole, which is shorter than its diff:
```python
import functools
import math

import jax
import jax.numpy as jnp
from jax import lax
from jax.experimental import pallas as pl
from jax.experimental.pallas import tpu as pltpu
from jax.sharding import PartitionSpec as P

CLIP_LIMIT = 64.0
MAX_CHUNKS = 4
ROWS_AT_ONCE = 2
VMEM_LIMIT = 66 * 1000 * 1000
MESH = pl.DeviceIdType.MESH
NT = (((1,), (1,)), ((), ()))
NN = (((1,), (0,)), ((), ()))
F32 = jnp.float32
BF16 = jnp.bfloat16


def dot(a, b, dims):
    return lax.dot_general(a, b, dims, preferred_element_type=F32)


def eye(n):
    rows = lax.broadcasted_iota(jnp.int32, (n, n), 0)
    cols = lax.broadcasted_iota(jnp.int32, (n, n), 1)
    return jnp.where(rows == cols, 1.0, 0.0).astype(BF16)


class Sizes:
    def __init__(self, na, nz, nh, rows, cols, depth, ch):
        self.na, self.nz, self.nh = na, nz, nh
        self.rb, self.k, self.d, self.ch = rows, cols, depth, ch
        self.g = na * nh
        self.naz = na * nz
        self.rh = rows // nh
        self.hid = ch * nh
        self.cp = ch // na
        self.nq = math.gcd(self.cp, MAX_CHUNKS)
        self.cq = self.cp // self.nq
        self.m = na * self.cq
        self.nc = self.g * self.cq
        self.i = na * rows
        self.br = math.gcd(self.rh, 16)
        self.nb = self.rh // self.br
        self.bi = math.gcd(self.rb, 16)
        self.sp = self.hid + 8
        self.pp = self.m + 8
        self.tp = self.br + 8
        self.tb = math.gcd(self.br // 2, ROWS_AT_ONCE)
        self.rs = 4 * self.m // self.naz


def kernel(s, p_ref, x_hbm, w_ref, gain_ref, mask_ref, mask_s, out_ref, wg_ref,
           xv, pt, pg, wall, wt, gain, unit_s, inv_s, nt_s, pr, fac, relay, lrs, lrb, gs, gr, turn, ng,
           raw, rx1, mine_s, rx2, rx3, sq,
           xsem, wsend, wrecv, psend, precv, zsend, zrecv, lsend, lrecv, gsend, grecv, osend, orecv,
           r1s, r1r, r2s, r2r, r3s, r3r, qs, qr):
    na, nz, nh, g_n, nq, cq, nc = s.na, s.nz, s.nh, s.g, s.nq, s.cq, s.nc
    rb, rh, k, d, ch, hid, br, nb, m = s.rb, s.rh, s.k, s.d, s.ch, s.hid, s.br, s.nb, s.m
    a, z, h = lax.axis_index("ia"), lax.axis_index("ja"), lax.axis_index("col")
    me_g = h * na + a
    me_n = a * nz + z
    row0 = a * rb + h * rh

    def plane(g):
        return (lax.rem(g, na), z, lax.div(g, na))

    def peer_g(step):
        return lax.rem(me_g + step, g_n)

    def send(src, dst, send_sem, recv_sem, device):
        return pltpu.make_async_remote_copy(
            src_ref=src, dst_ref=dst, send_sem=send_sem, recv_sem=recv_sem,
            device_id=device, device_id_type=MESH)

    barrier = pltpu.get_barrier_semaphore()
    total = s.naz * nh
    for step in range(1, total):
        to = lax.rem(me_n * nh + h + step, total)
        device = (lax.div(to, nz * nh), lax.rem(lax.div(to, nh), nz), lax.rem(to, nh))
        pl.semaphore_signal(barrier, inc=1, device_id=device, device_id_type=MESH)
    xcopy = pltpu.make_async_copy(x_hbm.at[pl.ds(h * rh, rh)], xv, xsem)
    xcopy.start()

    def p_turn(q):
        def block(ib, carry):
            slot = lax.rem(ib, 2)
            for ii in range(s.bi):
                relay[slot, ii * s.pp:ii * s.pp + m, :] = p_ref[ib * s.bi + ii, q * m:(q + 1) * m, :].astype(F32)
            for c in range(m):
                tile = relay[slot, pl.ds(c, s.bi, stride=s.pp), :]
                pt[q * m + c, pl.ds(pl.multiple_of(ib * s.bi, s.bi), s.bi), :] = tile.astype(BF16)
            return carry
        lax.fori_loop(0, rb // s.bi, block, 0)

    def p_copy(q, step):
        to = lax.rem(a + step, na)
        return send(pt.at[pl.ds(q * m + to * cq, cq)], pg.at[z, pl.ds(q * cq, cq), pl.ds(a * rb, rb)],
                    psend.at[q, step], precv.at[q, step], (to, z, h))

    def w_copy(step):
        return send(w_ref, wall.at[h], wsend.at[step], wrecv.at[step], (a, z, lax.rem(h + step, nh)))

    p_turn(0)
    pl.semaphore_wait(barrier, total - 1)
    for step in range(1, nh):
        w_copy(step).start()
    for q in range(nq):
        if q:
            p_turn(q)
        for step in range(1, na):
            p_copy(q, step).start()
    for q in range(nq):
        for r in range(cq):
            pg[z, q * cq + r, pl.ds(a * rb, rb), :] = pt[q * m + a * cq + r]

    def z_copy(q, block, up):
        ref = pg.at[block, pl.ds(q * cq, cq)]
        return send(ref, ref, zsend.at[q, block, 0 if up else 1], zrecv.at[q, block],
                    (a, z + 1 if up else z - 1, h))

    def z_own(q):
        for step in range(1, na):
            p_copy(q, step).wait_recv()

        @pl.when(z < nz - 1)
        def _():
            z_copy(q, z, True).start()

        @pl.when(z > 0)
        def _():
            z_copy(q, z, False).start()

    def z_hop(q, hop):
        @pl.when(z >= hop)
        def _():
            z_copy(q, z - hop, True).wait_recv()

            @pl.when(z < nz - 1)
            def _():
                z_copy(q, z - hop, True).start()

        @pl.when(z + hop < nz)
        def _():
            z_copy(q, z + hop, False).wait_recv()

            @pl.when(z > 0)
            def _():
                z_copy(q, z + hop, False).start()

    eye_d = eye(d)
    column = jnp.transpose(jnp.broadcast_to(gain_ref[...], (k, d)))
    gain[...] = jnp.concatenate([column, column], axis=1)
    wall[h] = w_ref[...]
    for step in range(1, nh):
        w_copy(step).wait_recv()
    for q in range(nq):
        rows = [wall[half, w, q * m:(q + 1) * m, :] for half in range(nh) for w in range(4)]
        wt[q] = dot(eye_d, jnp.concatenate(rows, axis=0), NT).astype(BF16)

    xcopy.wait()
    col_valid = mask_ref[pl.ds(z, 1), :].astype(F32)

    def rows_step(t, sub):
        x2 = xv[pl.ds(2 * t, 2)].reshape(2 * k, d)
        xt = dot(eye_d, x2, NT)
        centred = xt - jnp.mean(xt, axis=0, keepdims=True)
        inv = lax.rsqrt(jnp.mean(centred * centred, axis=0, keepdims=True) + 1e-05)
        unit = centred * inv
        normed = (unit * gain[...]).astype(BF16)
        unit_s[t] = unit
        inv_s[t] = inv
        nt_s[t] = normed
        for half in range(nh):
            pr[half * 4 * ch:(half + 1) * 4 * ch, :] = dot(wall[half].reshape(4 * ch, d), normed, NN)
        valid = jnp.concatenate(
            [col_valid * mask_s[row0 + 2 * t + e].astype(F32) for e in range(2)], axis=1)
        for q in range(nq):
            for side in range(2):
                def part(w):
                    at = [half * 4 * ch + w * ch + q * m for half in range(nh)]
                    return jnp.concatenate([pr[x:x + m, :] for x in at], axis=0)
                lin = part(2 * side)
                gate = jax.nn.sigmoid(part(2 * side + 1))
                first = valid * gate
                value = first * lin
                fac[t, q, 2 * side] = first.astype(BF16)
                fac[t, q, 2 * side + 1] = (value * (1.0 - gate)).astype(BF16)
                for e in range(2):
                    at = pl.multiple_of((2 * sub + e) * s.sp, 8) + q * nc
                    relay[side, pl.ds(at, nc), :] = value[:, e * k:(e + 1) * k]

    for b in range(nb):
        def one(sub, carry, b=b):
            rows_step(b * (br // 2) + sub, sub)
            return carry
        lax.fori_loop(0, br // 2, one, 0)

        def flush(c, carry, b=b):
            for side in range(2):
                tile = relay[side, pl.ds(c, br, stride=s.sp), :]
                lrs[side, c, b * br:(b + 1) * br, :] = tile.astype(BF16)
            return carry
        lax.fori_loop(0, hid, flush, 0, unroll=4)
        if b < nq:
            z_own(b)
    for q in range(nb, nq):
        z_own(q)

    def lr_copy(q, step):
        return send(lrs.at[:, pl.ds(q * nc + peer_g(step) * cq, cq)],
                    lrb.at[:, pl.ds(q * cq, cq), pl.ds(row0, rh)],
                    lsend.at[q, step], lrecv.at[q, step], plane(peer_g(step)))

    for q in range(nq):
        for step in range(1, g_n):
            lr_copy(q, step).start()
    for q in range(nq):
        for side in range(2):
            for r in range(cq):
                lrb[side, q * cq + r, pl.ds(row0, rh), :] = lrs[side, q * nc + me_g * cq + r]

    eye_k = eye(k)

    def triangle(c):
        panel = jnp.concatenate([pg[b, c] for b in range(nz)], axis=1)
        left, right = lrb[0, c], lrb[1, c]
        gs[0, c] = dot(panel, right, NN).astype(BF16)
        left_t = dot(eye_k, left, NT).astype(BF16)
        back_t = dot(left_t, panel, NN).astype(BF16)
        for b in range(nz):
            gs[1, c, b * k:(b + 1) * k, :] = dot(eye_k, back_t[:, b * k:(b + 1) * k], NT).astype(BF16)

    def g_copy(q, b, step):
        g = peer_g(step)
        row = lax.rem(g, na) * rb + lax.div(g, na) * rh + b * br
        return send(gs.at[:, pl.ds(q * cq, cq), pl.ds(row, br)],
                    gr.at[:, pl.ds(q * nc + me_g * cq, cq), pl.ds(b * br, br)],
                    gsend.at[q, b, step], grecv.at[q, b, step], plane(g))

    def out_copy(b, step):
        ref = out_ref.at[pl.ds(h * rh + b * br, br)]
        return send(ref, ref, osend.at[b, step], orecv.at[b, step], (a, z, lax.rem(h + step, nh)))

    def r1_copy(q, step):
        to = lax.rem(h + step, nh)
        return send(raw.at[q, to], rx1.at[q, step], r1s.at[q, step], r1r.at[q, step], (a, z, to))

    def r1_sum(q):
        mine = raw[q, h]
        for step in range(1, nh):
            r1_copy(q, step).wait_recv()
            mine = mine + rx1[q, step]
        for n in range(s.naz):
            mine_s[n, q] = mine[n * s.rs:(n + 1) * s.rs]

    def peer_n(step):
        return lax.rem(me_n + step, s.naz)

    def at_n(n):
        return (lax.div(n, nz), lax.rem(n, nz), h)

    batches = [(0, nq - 1), (nq - 1, nq)] if nq > 1 else [(0, nq)]

    def r2_copy(batch, step):
        lo, hi = batches[batch]
        n = peer_n(step)
        return send(mine_s.at[n, lo:hi], rx2.at[step, lo:hi], r2s.at[batch, step], r2r.at[batch, step], at_n(n))

    def r2_sum(batch):
        lo, hi = batches[batch]
        mine = mine_s[me_n, lo:hi]
        for step in range(1, s.naz):
            r2_copy(batch, step).wait_recv()
            mine = mine + rx2[step, lo:hi]
        rx3[me_n, lo:hi] = mine

    def r3_copy(batch, step):
        lo, hi = batches[batch]
        ref = rx3.at[me_n, lo:hi]
        return send(ref, ref, r3s.at[batch, step], r3r.at[batch, step], at_n(peer_n(step)))

    def sq_copy(step):
        return send(sq.at[0], sq.at[step], qs.at[step], qr.at[step], (a, z, lax.rem(h + step, nh)))

    def gather(q, b):
        for step in range(1, g_n):
            g_copy(q, b, step).wait_recv()

        def spread(n, carry):
            for side in range(2):
                tile = gr[side, q * nc + n, b * br:(b + 1) * br, :].astype(F32)
                turn[side, pl.ds(pl.multiple_of(n * s.tp, 8), br), :] = tile
            return carry
        lax.fori_loop(0, nc, spread, 0, unroll=4)
        if b == 0:
            raw[q] = jnp.zeros((nh, 4 * m, d), F32)

        def one(sub, carry):
            t0 = b * (br // 2) + sub * s.tb
            terms = []
            for side in range(2):
                both = jnp.concatenate(
                    [turn[side, pl.ds(2 * s.tb * sub + e, nc, stride=s.tp), :] for e in range(2 * s.tb)], axis=1)
                for w in range(2):
                    factor = jnp.concatenate([fac[t0 + u, q, 2 * side + w] for u in range(s.tb)], axis=1)
                    terms.append((both * factor.astype(F32)).astype(BF16))
            grads = jnp.concatenate(
                [term[half * m:(half + 1) * m] for half in range(nh) for term in terms], axis=0)
            normed = jnp.concatenate([nt_s[t0 + u] for u in range(s.tb)], axis=1)
            raw[q] += dot(grads, normed, NT).reshape(nh, 4 * m, d)
            part = dot(wt[q], grads, NN)
            for u in range(s.tb):
                piece = part[:, u * 2 * k:(u + 1) * 2 * k]
                ng[t0 + u] = ng[t0 + u] + piece if q else piece
            return carry
        lax.fori_loop(0, br // 2 // s.tb, one, 0)

    def norm_back(b):
        def one(sub, carry):
            t = b * (br // 2) + sub
            unit = unit_s[t]
            scaled = ng[t] * gain[...]
            first = jnp.mean(scaled, axis=0, keepdims=True)
            second = jnp.mean(scaled * unit, axis=0, keepdims=True)
            res = (inv_s[t] * (scaled - first - unit * second)).astype(BF16)
            for e in range(2):
                out_ref[h * rh + 2 * t + e] = dot(eye_k, res[:, e * k:(e + 1) * k], NT).astype(BF16)
            return carry
        lax.fori_loop(0, br // 2, one, 0, unroll=2)
        for step in range(1, nh):
            out_copy(b, step).start()

    for hop in range(1, nz - 1):
        for q in range(nq):
            z_hop(q, hop)
    for q in range(nq):
        z_hop(q, nz - 1)
        for step in range(1, g_n):
            lr_copy(q, step).wait_recv()

        def tri(r, carry, q=q):
            triangle(q * cq + r)
            return carry
        lax.fori_loop(0, cq, tri, 0)
        for b in range(nb):
            for step in range(1, g_n):
                g_copy(q, b, step).start()
        for side in range(2):
            for r in range(cq):
                gr[side, q * nc + me_g * cq + r] = gs[side, q * cq + r, pl.ds(row0, rh), :]
        if q:
            for b in range(nb):
                gather(q - 1, b)
            for step in range(1, nh):
                r1_copy(q - 1, step).start()
    if nq > 1:
        for q in range(nq - 1):
            r1_sum(q)
        for step in range(1, s.naz):
            r2_copy(0, step).start()
    last = nq - 1
    for b in range(nb):
        gather(last, b)
        if b == nb - 1:
            for step in range(1, nh):
                r1_copy(last, step).start()
        if b == 0 and nq > 1:
            r2_sum(0)
            for step in range(1, s.naz):
                r3_copy(0, step).start()
        if b < nb - 1:
            norm_back(b)
    r1_sum(last)
    end = len(batches) - 1
    for step in range(1, s.naz):
        r2_copy(end, step).start()
    norm_back(nb - 1)
    r2_sum(end)
    for step in range(1, s.naz):
        r3_copy(end, step).start()
    for batch in range(len(batches)):
        for step in range(1, s.naz):
            r3_copy(batch, step).wait_recv()
    found = rx3[...].reshape(s.naz * nq, s.rs, d)
    row = jnp.sum(jnp.sum(found * found, axis=0), axis=0, keepdims=True)
    sq[0] = jnp.broadcast_to(row, (8, d))
    for step in range(1, nh):
        sq_copy(step).start()
    for step in range(1, nh):
        sq_copy(step).wait()
    squares = jnp.sum(jnp.sum(sq[...], axis=0)[0:1, :], axis=1, keepdims=True)
    factor = jnp.minimum(1.0, CLIP_LIMIT * lax.rsqrt(squares + 1e-06))
    for q in range(nq):
        full = jnp.concatenate([rx3[n, q] for n in range(s.naz)], axis=0) * factor
        for w in range(4):
            wg_ref[w, q * m:(q + 1) * m, :] = full[w * m:(w + 1) * m]

    for b in range(nb):
        for step in range(1, nh):
            out_copy(b, step).wait()
    for step in range(1, nh):
        w_copy(step).wait_send()
    for batch in range(len(batches)):
        for step in range(1, s.naz):
            r2_copy(batch, step).wait_send()
            r3_copy(batch, step).wait_send()
    for q in range(nq):
        for step in range(1, nh):
            r1_copy(q, step).wait_send()
        for step in range(1, na):
            p_copy(q, step).wait_send()
        for step in range(1, g_n):
            lr_copy(q, step).wait_send()
            for b in range(nb):
                g_copy(q, b, step).wait_send()
        for hop in range(nz):
            @pl.when((z >= hop) & (z < nz - 1))
            def _(q=q, hop=hop):
                z_copy(q, z - hop, True).wait_send()

            @pl.when((z + hop < nz) & (z > 0))
            def _(q=q, hop=hop):
                z_copy(q, z + hop, False).wait_send()


def on_device(na, nz, nh, pair_rep, norm_gain, weights, residue_mask, product_grad):
    rows, cols, depth = pair_rep.shape
    ch = product_grad.shape[1]
    s = Sizes(na, nz, nh, rows, cols, depth, ch)
    vm = pl.BlockSpec(memory_space=pltpu.VMEM)
    dma = pltpu.SemaphoreType.DMA
    half = s.rh // 2
    slices = (s.naz, s.nq, s.rs, depth)
    scratch = [
        pltpu.VMEM((s.rh, cols, depth), BF16),
        pltpu.VMEM((ch, rows, cols), BF16),
        pltpu.VMEM((nz, s.cp, s.i, cols), BF16),
        pltpu.VMEM((nh, 4, ch, depth), BF16),
        pltpu.VMEM((s.nq, depth, 4 * s.nc), BF16),
        pltpu.VMEM((depth, 2 * cols), F32),
        pltpu.VMEM((half, depth, 2 * cols), F32),
        pltpu.VMEM((half, 1, 2 * cols), F32),
        pltpu.VMEM((half, depth, 2 * cols), BF16),
        pltpu.VMEM((4 * s.hid, 2 * cols), F32),
        pltpu.VMEM((half, s.nq, 4, s.nc, 2 * cols), BF16),
        pltpu.VMEM((2, max(s.br * s.sp, s.bi * s.pp), cols), F32),
        pltpu.VMEM((2, s.hid, s.rh, cols), BF16),
        pltpu.VMEM((2, s.cp, s.i, cols), BF16),
        pltpu.VMEM((2, s.cp, s.i, cols), BF16),
        pltpu.VMEM((2, s.hid, s.rh, cols), BF16),
        pltpu.VMEM((2, s.nc * s.tp, cols), F32),
        pltpu.VMEM((half, depth, 2 * cols), F32),
        pltpu.VMEM((s.nq, nh, 4 * s.m, depth), F32),
        pltpu.VMEM((s.nq, nh, 4 * s.m, depth), F32),
        pltpu.VMEM(slices, F32),
        pltpu.VMEM(slices, F32),
        pltpu.VMEM(slices, F32),
        pltpu.VMEM((nh, 8, depth), F32),
        dma(()), dma((nh,)), dma((nh,)),
        dma((s.nq, na)), dma((s.nq, na)), dma((s.nq, nz, 2)), dma((s.nq, nz)),
        dma((s.nq, s.g)), dma((s.nq, s.g)), dma((s.nq, s.nb, s.g)), dma((s.nq, s.nb, s.g)),
        dma((s.nb, nh)), dma((s.nb, nh)),
        dma((s.nq, nh)), dma((s.nq, nh)), dma((2, s.naz)), dma((2, s.naz)), dma((2, s.naz)), dma((2, s.naz)),
        dma((nh,)), dma((nh,)),
    ]
    pair_grad, found = pl.pallas_call(
        functools.partial(kernel, s),
        out_shape=(
            jax.ShapeDtypeStruct((rows, cols, depth), BF16),
            jax.ShapeDtypeStruct((4, ch, depth), F32),
        ),
        in_specs=[vm, pl.BlockSpec(memory_space=pl.ANY), vm, vm, vm, pl.BlockSpec(memory_space=pltpu.SMEM)],
        out_specs=(vm, vm),
        scratch_shapes=scratch,
        compiler_params=pltpu.CompilerParams(
            collective_id=0, has_side_effects=True, vmem_limit_bytes=VMEM_LIMIT),
    )(product_grad, pair_rep, weights.transpose(0, 2, 1), norm_gain.reshape(1, depth),
      residue_mask.reshape(nz, cols), residue_mask)
    return (pair_grad, found.transpose(0, 2, 1))


def solution(mesh):
    sizes = mesh.shape["ia"], mesh.shape["ja"], mesh.shape["col"]
    placed = (P("ia", "ja", None), P(), P(None, None, "col"), P(), P("ia", "col", "ja"))

    def step(*args):
        return on_device(*sizes, *args)

    return jax.shard_map(
        step,
        mesh=mesh,
        in_specs=placed,
        out_specs=(P("ia", "ja", None), P(None, None, "col")),
        check_vma=False,
    )
```

time: 230 us -> 198 us (0.86)
  waiting for transfers between devices: 20.9 us -> 0 us
  Pallas kernels: 182 us -> 192 us
  local copies, waits for them, and re-layouts: 12.7 us -> 5.48 us
  blocking collectives: 5.33 us -> 0 us
  starting transfers between devices: 4.17 us -> 0 us
  other arithmetic: 2.68 us -> 0 us
    ppermute x5 -> x0, waiting for transfers between devices: 20.9 us -> none  [exchange(): lax.ppermute(value, axis, [(a, partner(a, step, count)) for a in range(co...]
    pallas_call x1, Pallas kernels: 182 us -> 192 us  [on_device(): pl.pallas_call(functools.partial(kernel, s), out_shape=(jax.ShapeDtypeStr...]
    transpose x1 -> x0, local copies, waits for them, and re-layouts: 4.26 us -> none  [on_device(): panels = product_grad.transpose(1, 0, 2).reshape(na, s.nq, s.cq, rows, cols)]
    ppermute x5 -> x0, starting transfers between devices: 4.17 us -> none  [exchange(): lax.ppermute(value, axis, [(a, partner(a, step, count)) for a in range(co...]
    psum x1 -> x0, blocking collectives: 3.08 us -> none  [on_device(): squares = lax.psum(jnp.sum(summed * summed), 'col')]
    reshape x4 -> x0, local copies, waits for them, and re-layouts: 2.52 us -> none  [the longest x1 1 us: on_device(): raw = raw.reshape(s.nq, 4, nh, na, s.cq, depth)]
    unnamed x3 -> x4, local copies, waits for them, and re-layouts: 4.79 us -> 5.48 us
  transfers between devices with their start and end apart: 5 -> 0, of which waited for: 5 -> 0; matrix products, arithmetic and copies ran while one was open for 0% -> 0% of each run, Pallas kernels for 0% -> 0%
where the time goes in v1:
time: 198 us
  Pallas kernels  192 us (97%)
  local copies, waits for them, and re-layouts  5.48 us (3%)
    pallas_call x1, Pallas kernels, on_device(): pl.pallas_call(functools.partial(kernel, s), out_shape=(jax.ShapeDtypeStr...  192 us
    unnamed x4, local copies, waits for them, and re-layouts  5.48 us

profile of v1, /device:TPU:0, one launch (start us, length us, event | category | flops | bytes accessed | tf_op | source)
XLA Modules:
  0.0 198.2 jit_solution(462134806826537835)
XLA Ops:
  0.6 192.1 %shard_map.68 = (bf16[128,128,128]{2,1,0:T(8,128)(2,1)}, f32[4,64,128]{2,1,0:T(8,128)}) custom-call(bf16[128,64,128]{2,1,0:T(8,128)(2,1)} %p_ref.1, bf16[128,128,128]{2,1,0:T(8,128)(2,1)} %x_hbm.1, bf16[4,64,128]{2,1,0:T(8,128)(2,1)} %bitcast.5, f32[1,128]{1,0:T(1,128)} %bitcast.7, s32[4,128]{1,0:T(4,128)} %bitcast.6, s32[512]{0:T(512)} %mask_s.1), custom_call_target="tpu_custom_call" | custom-call | tf_op jit(solution)/shard_map/pallas_call | solution.py:470
  192.7 0.0 copy-start
  192.7 4.8 %copy.9 = bf16[128,128,128]{2,1,0:T(8,128)(2,1)} copy(bf16[128,128,128]{2,1,0:T(8,128)(2,1)} %get-tuple-element.8) | data formatting | bytes 8388608
  197.6 0.0 copy-done
  197.6 0.7 copy.10
Async XLA Ops:
  192.7 4.8 %copy-start = (f32[4,64,128]{2,1,0:T(8,128)S(1)}, f32[4,64,128]{2,1,0:T(8,128)}, u32[]{:S(2)}) copy-start(f32[4,64,128]{2,1,0:T(8,128)} %get-tuple-element.5) | copy-start | bytes 393220

commit v2 on v1

--- a/solution.py
+++ b/solution.py
@@ -51,19 +51,26 @@
         self.tp = self.br + 8
         self.tb = math.gcd(self.br // 2, ROWS_AT_ONCE)
         self.rs = 4 * self.m // self.naz
+        self.q0 = self.nq - self.nq // 2 if nz > 3 else self.nq
+        self.helped = max(self.nq - self.q0, 1)
 
 
 def kernel(s, p_ref, x_hbm, w_ref, gain_ref, mask_ref, mask_s, out_ref, wg_ref,
-           xv, pt, pg, wall, wt, gain, unit_s, inv_s, nt_s, pr, fac, relay, lrs, lrb, gs, gr, turn, ng,
+           xv, pt, pg, wall, wt, gain, unit_s, inv_s, nt_s, pr, fac, relay, lrs, lrb, lrh, gs, gsh, gr, turn, ng,
            raw, rx1, mine_s, rx2, rx3, sq,
            xsem, wsend, wrecv, psend, precv, zsend, zrecv, lsend, lrecv, gsend, grecv, osend, orecv,
-           r1s, r1r, r2s, r2r, r3s, r3r, qs, qr):
+           r1s, r1r, r2s, r2r, r3s, r3r, qs, qr, hls, hlr, hgs, hgr):
     na, nz, nh, g_n, nq, cq, nc = s.na, s.nz, s.nh, s.g, s.nq, s.cq, s.nc
     rb, rh, k, d, ch, hid, br, nb, m = s.rb, s.rh, s.k, s.d, s.ch, s.hid, s.br, s.nb, s.m
     a, z, h = lax.axis_index("ia"), lax.axis_index("ja"), lax.axis_index("col")
     me_g = h * na + a
     me_n = a * nz + z
     row0 = a * rb + h * rh
+    q0 = s.q0
+    is_end = (z == 0) | (z == nz - 1)
+    is_near = (z == 1) | (z == nz - 2)
+    inward = jnp.where(z == 0, 1, nz - 2)
+    outward = jnp.where(z == 1, 0, nz - 1)
 
     def plane(g):
         return (lax.rem(g, na), z, lax.div(g, na))
@@ -122,34 +129,46 @@
         return send(ref, ref, zsend.at[q, block, 0 if up else 1], zrecv.at[q, block],
                     (a, z + 1 if up else z - 1, h))
 
+    def goes_up(q):
+        return z < (nz - 1 if q < q0 else nz - 2)
+
+    def goes_down(q):
+        return z > (0 if q < q0 else 1)
+
     def z_own(q):
         for step in range(1, na):
             p_copy(q, step).wait_recv()
 
-        @pl.when(z < nz - 1)
+        @pl.when(goes_up(q))
         def _():
             z_copy(q, z, True).start()
 
-        @pl.when(z > 0)
+        @pl.when(goes_down(q))
         def _():
             z_copy(q, z, False).start()
 
-    def z_hop(q, hop):
-        @pl.when(z >= hop)
+    def z_forward(q, hop):
+        @pl.when((z >= hop) & goes_up(q))
         def _():
             z_copy(q, z - hop, True).wait_recv()
-
-            @pl.when(z < nz - 1)
-            def _():
-                z_copy(q, z - hop, True).start()
-
-        @pl.when(z + hop < nz)
+            z_copy(q, z - hop, True).start()
+
+        @pl.when((z + hop < nz) & goes_down(q))
         def _():
             z_copy(q, z + hop, False).wait_recv()
-
-            @pl.when(z > 0)
-            def _():
-                z_copy(q, z + hop, False).start()
+            z_copy(q, z + hop, False).start()
+
+    def z_rest(q):
+        for hop in range(1, nz):
+            here = True if q < q0 else jnp.logical_not(is_end)
+
+            @pl.when((z >= hop) & jnp.logical_not(goes_up(q)) & here)
+            def _(hop=hop):
+                z_copy(q, z - hop, True).wait_recv()
+
+            @pl.when((z + hop < nz) & jnp.logical_not(goes_down(q)) & here)
+            def _(hop=hop):
+                z_copy(q, z + hop, False).wait_recv()
 
     eye_d = eye(d)
     column = jnp.transpose(jnp.broadcast_to(gain_ref[...], (k, d)))
@@ -205,17 +224,22 @@
                 lrs[side, c, b * br:(b + 1) * br, :] = tile.astype(BF16)
             return carry
         lax.fori_loop(0, hid, flush, 0, unroll=4)
-        if b < nq:
+        if b < q0:
             z_own(b)
-    for q in range(nb, nq):
+    for q in range(nb, q0):
         z_own(q)
+
+    @pl.when(is_end)
+    def _():
+        for q in range(q0, nq):
+            z_own(q)
 
     def lr_copy(q, step):
         return send(lrs.at[:, pl.ds(q * nc + peer_g(step) * cq, cq)],
                     lrb.at[:, pl.ds(q * cq, cq), pl.ds(row0, rh)],
                     lsend.at[q, step], lrecv.at[q, step], plane(peer_g(step)))
 
-    for q in range(nq):
+    for q in [*range(q0, nq), *range(q0)]:
         for step in range(1, g_n):
             lr_copy(q, step).start()
     for q in range(nq):
@@ -225,19 +249,34 @@
 
     eye_k = eye(k)
 
-    def triangle(c):
+    def triangle(c, lr, at, to):
         panel = jnp.concatenate([pg[b, c] for b in range(nz)], axis=1)
-        left, right = lrb[0, c], lrb[1, c]
-        gs[0, c] = dot(panel, right, NN).astype(BF16)
+        left, right = lr[0, at], lr[1, at]
+        to[0, at] = dot(panel, right, NN).astype(BF16).reshape(g_n, rh, k)
         left_t = dot(eye_k, left, NT).astype(BF16)
         back_t = dot(left_t, panel, NN).astype(BF16)
-        for b in range(nz):
-            gs[1, c, b * k:(b + 1) * k, :] = dot(eye_k, back_t[:, b * k:(b + 1) * k], NT).astype(BF16)
+        back = [dot(eye_k, back_t[:, b * k:(b + 1) * k], NT).astype(BF16) for b in range(nz)]
+        to[1, at] = jnp.concatenate(back, axis=0).reshape(g_n, rh, k)
+
+    def triangles(q, lr, to, base):
+        def one(r, carry):
+            triangle(q * cq + r, lr, (q - base) * cq + r, to)
+            return carry
+        lax.fori_loop(0, cq, one, 0)
+
+    def in_copy(q, z_to):
+        return send(lrb.at[:, pl.ds(q * cq, cq)], lrh.at[:, pl.ds((q - q0) * cq, cq)],
+                    hls.at[q - q0], hlr.at[q - q0], (a, z_to, h))
+
+    def back_copy(q, b, z_to):
+        return send(gsh.at[:, pl.ds((q - q0) * cq, cq), :, pl.ds(b * br, br)],
+                    gs.at[:, pl.ds(q * cq, cq), :, pl.ds(b * br, br)],
+                    hgs.at[q - q0, b], hgr.at[q - q0, b], (a, z_to, h))
 
     def g_copy(q, b, step):
         g = peer_g(step)
-        row = lax.rem(g, na) * rb + lax.div(g, na) * rh + b * br
-        return send(gs.at[:, pl.ds(q * cq, cq), pl.ds(row, br)],
+        place = lax.rem(g, na) * nh + lax.div(g, na)
+        return send(gs.at[:, pl.ds(q * cq, cq), place, pl.ds(b * br, br)],
                     gr.at[:, pl.ds(q * nc + me_g * cq, cq), pl.ds(b * br, br)],
                     gsend.at[q, b, step], grecv.at[q, b, step], plane(g))
 
@@ -334,27 +373,89 @@
         for step in range(1, nh):
             out_copy(b, step).start()
 
-    for hop in range(1, nz - 1):
-        for q in range(nq):
-            z_hop(q, hop)
-    for q in range(nq):
-        z_hop(q, nz - 1)
+    def lr_wait(q):
         for step in range(1, g_n):
             lr_copy(q, step).wait_recv()
 
-        def tri(r, carry, q=q):
-            triangle(q * cq + r)
-            return carry
-        lax.fori_loop(0, cq, tri, 0)
-        for b in range(nb):
-            for step in range(1, g_n):
-                g_copy(q, b, step).start()
+    def g_send(q, b):
+        for step in range(1, g_n):
+            g_copy(q, b, step).start()
         for side in range(2):
             for r in range(cq):
-                gr[side, q * nc + me_g * cq + r] = gs[side, q * cq + r, pl.ds(row0, rh), :]
+                gr[side, q * nc + me_g * cq + r, b * br:(b + 1) * br, :] = gs[
+                    side, q * cq + r, a * nh + h, b * br:(b + 1) * br, :]
+
+    def make(q):
+        if q < q0:
+            z_rest(q)
+            lr_wait(q)
+            triangles(q, lrb, gs, 0)
+            return
+
+        @pl.when(is_near)
+        def _():
+            z_rest(q)
+            in_copy(q, outward).wait_recv()
+            triangles(q, lrh, gsh, q0)
+            for b in range(nb):
+                back_copy(q, b, outward).start()
+            lr_wait(q)
+            triangles(q, lrb, gs, 0)
+
+        @pl.when(jnp.logical_not(is_near | is_end))
+        def _():
+            z_rest(q)
+            lr_wait(q)
+            triangles(q, lrb, gs, 0)
+
+    def came_back(q, b):
+        if q >= q0:
+            @pl.when(is_end)
+            def _():
+                back_copy(q, b, outward).wait_recv()
+
+    for hop in range(1, nz - 1):
+        for q in range(q0):
+            z_forward(q, hop)
+        if hop == 1 and q0 < nq:
+            @pl.when(jnp.logical_not(is_end))
+            def _():
+                z_own(q0)
+    for q in range(q0, nq):
+        for hop in range(1, nz - 1):
+            z_forward(q, hop)
+        if q + 1 < nq:
+            @pl.when(jnp.logical_not(is_end))
+            def _(q=q):
+                z_own(q + 1)
+
+    @pl.when(is_end)
+    def _():
+        for q in range(q0, nq):
+            lr_wait(q)
+            in_copy(q, inward).start()
+
+    last = nq - 1
+    late = 0
+    before = []
+    for q in range(nq):
+        make(q)
+        for b in range(nb):
+            came_back(q, b)
+            g_send(q, b)
+            for _ in range(2):
+                if before:
+                    gather(*before.pop(0))
+            if q == last and not before and b > 1:
+                at = b - 2 - late
+                gather(last, at)
+                norm_back(at)
+            elif q == last and b > 1:
+                late += 1
+        for task in before:
+            gather(*task)
+        before = [(q, b) for b in range(nb)]
         if q:
-            for b in range(nb):
-                gather(q - 1, b)
             for step in range(1, nh):
                 r1_copy(q - 1, step).start()
     if nq > 1:
@@ -362,17 +463,16 @@
             r1_sum(q)
         for step in range(1, s.naz):
             r2_copy(0, step).start()
-    last = nq - 1
-    for b in range(nb):
+    for b in range(max(nb - 2 - late, 0), nb):
         gather(last, b)
         if b == nb - 1:
             for step in range(1, nh):
                 r1_copy(last, step).start()
-        if b == 0 and nq > 1:
-            r2_sum(0)
-            for step in range(1, s.naz):
-                r3_copy(0, step).start()
-        if b < nb - 1:
+            if nq > 1:
+                r2_sum(0)
+                for step in range(1, s.naz):
+                    r3_copy(0, step).start()
+        else:
             norm_back(b)
     r1_sum(last)
     end = len(batches) - 1
@@ -418,13 +518,22 @@
             for b in range(nb):
                 g_copy(q, b, step).wait_send()
         for hop in range(nz):
-            @pl.when((z >= hop) & (z < nz - 1))
+            @pl.when((z >= hop) & goes_up(q))
             def _(q=q, hop=hop):
                 z_copy(q, z - hop, True).wait_send()
 
-            @pl.when((z + hop < nz) & (z > 0))
+            @pl.when((z + hop < nz) & goes_down(q))
             def _(q=q, hop=hop):
                 z_copy(q, z + hop, False).wait_send()
+        if q >= q0:
+            @pl.when(is_end)
+            def _(q=q):
+                in_copy(q, inward).wait_send()
+
+            @pl.when(is_near)
+            def _(q=q):
+                for b in range(nb):
+                    back_copy(q, b, outward).wait_send()
 
 
 def on_device(na, nz, nh, pair_rep, norm_gain, weights, residue_mask, product_grad):
@@ -450,7 +559,9 @@
         pltpu.VMEM((2, max(s.br * s.sp, s.bi * s.pp), cols), F32),
         pltpu.VMEM((2, s.hid, s.rh, cols), BF16),
         pltpu.VMEM((2, s.cp, s.i, cols), BF16),
-        pltpu.VMEM((2, s.cp, s.i, cols), BF16),
+        pltpu.VMEM((2, s.helped * s.cq, s.i, cols), BF16),
+        pltpu.VMEM((2, s.cp, s.g, s.rh, cols), BF16),
+        pltpu.VMEM((2, s.helped * s.cq, s.g, s.rh, cols), BF16),
         pltpu.VMEM((2, s.hid, s.rh, cols), BF16),
         pltpu.VMEM((2, s.nc * s.tp, cols), F32),
         pltpu.VMEM((half, depth, 2 * cols), F32),
@@ -466,6 +577,7 @@
         dma((s.nb, nh)), dma((s.nb, nh)),
         dma((s.nq, nh)), dma((s.nq, nh)), dma((2, s.naz)), dma((2, s.naz)), dma((2, s.naz)), dma((2, s.naz)),
         dma((nh,)), dma((nh,)),
+        dma((s.helped,)), dma((s.helped,)), dma((s.helped, s.nb)), dma((s.helped, s.nb)),
     ]
     pair_grad, found = pl.pallas_call(
         functools.partial(kernel, s),

time: 198 us -> 173 us (0.87)
  Pallas kernels: 192 us -> 167 us
    pallas_call x1, Pallas kernels: 192 us -> 167 us  [on_device(): pl.pallas_call(functools.partial(kernel, s), out_shape=(jax.ShapeDtypeStr...]
where the time goes in v2:
time: 173 us
  Pallas kernels  167 us (97%)
  local copies, waits for them, and re-layouts  5.48 us (3%)
    pallas_call x1, Pallas kernels, on_device(): pl.pallas_call(functools.partial(kernel, s), out_shape=(jax.ShapeDtypeStr...  167 us
    unnamed x4, local copies, waits for them, and re-layouts  5.48 us

profile of v2, /device:TPU:0, one launch (start us, length us, event | category | flops | bytes accessed | tf_op | source)
XLA Modules:
  0.0 173.2 jit_solution(3807706765675046554)
XLA Ops:
  0.6 167.1 %shard_map.68 = (bf16[128,128,128]{2,1,0:T(8,128)(2,1)}, f32[4,64,128]{2,1,0:T(8,128)}) custom-call(bf16[128,64,128]{2,1,0:T(8,128)(2,1)} %p_ref.1, bf16[128,128,128]{2,1,0:T(8,128)(2,1)} %x_hbm.1, bf16[4,64,128]{2,1,0:T(8,128)(2,1)} %bitcast.5, f32[1,128]{1,0:T(1,128)} %bitcast.7, s32[4,128]{1,0:T(4,128)} %bitcast.6, s32[512]{0:T(512)} %mask_s.1), custom_call_target="tpu_custom_call" | custom-call | tf_op jit(solution)/shard_map/pallas_call | solution.py:582
  167.7 0.0 copy-start
  167.7 4.8 %copy.9 = bf16[128,128,128]{2,1,0:T(8,128)(2,1)} copy(bf16[128,128,128]{2,1,0:T(8,128)(2,1)} %get-tuple-element.8) | data formatting | bytes 8388608
  172.5 0.0 copy-done
  172.5 0.7 copy.10
Async XLA Ops:
  167.7 4.8 %copy-start = (f32[4,64,128]{2,1,0:T(8,128)S(1)}, f32[4,64,128]{2,1,0:T(8,128)}, u32[]{:S(2)}) copy-start(f32[4,64,128]{2,1,0:T(8,128)} %get-tuple-element.5) | copy-start | bytes 393220

commit v3 on v2

--- a/solution.py
+++ b/solution.py
@@ -50,16 +50,20 @@
         self.pp = self.m + 8
         self.tp = self.br + 8
         self.tb = math.gcd(self.br // 2, ROWS_AT_ONCE)
-        self.rs = 4 * self.m // self.naz
+        self.no = math.gcd(max(4 * self.m // 8, 1), self.naz)
+        self.rs = 4 * self.m // self.no
+        self.per = max(self.no // na, 1)
+        self.stride = na * self.per // self.no
+        self.base = (nz - self.per) // 2
         self.q0 = self.nq - self.nq // 2 if nz > 3 else self.nq
         self.helped = max(self.nq - self.q0, 1)
 
 
-def kernel(s, p_ref, x_hbm, w_ref, gain_ref, mask_ref, mask_s, out_ref, wg_ref,
+def kernel(s, p_ref, x_hbm, w_ref, gain_ref, mask_ref, mask_s, out_hbm, wg_ref,
            xv, pt, pg, wall, wt, gain, unit_s, inv_s, nt_s, pr, fac, relay, lrs, lrb, lrh, gs, gsh, gr, turn, ng,
-           raw, rx1, mine_s, rx2, rx3, sq,
+           outv, raw, rx1, mine_s, rx2, rx3, sq,
            xsem, wsend, wrecv, psend, precv, zsend, zrecv, lsend, lrecv, gsend, grecv, osend, orecv,
-           r1s, r1r, r2s, r2r, r3s, r3r, qs, qr, hls, hlr, hgs, hgr):
+           r1s, r1r, r2s, r2r, r3s, r3r, qs, qr, keep, hls, hlr, hgs, hgr):
     na, nz, nh, g_n, nq, cq, nc = s.na, s.nz, s.nh, s.g, s.nq, s.cq, s.nc
     rb, rh, k, d, ch, hid, br, nb, m = s.rb, s.rh, s.k, s.d, s.ch, s.hid, s.br, s.nb, s.m
     a, z, h = lax.axis_index("ia"), lax.axis_index("ja"), lax.axis_index("col")
@@ -103,10 +107,14 @@
             return carry
         lax.fori_loop(0, rb // s.bi, block, 0)
 
-    def p_copy(q, step):
+    def pieces(q):
+        return [(q * cq + r, 1) for r in range(cq)] if q == 0 else [(q * cq, cq)]
+
+    def p_copy(piece, step):
+        c, n = piece
         to = lax.rem(a + step, na)
-        return send(pt.at[pl.ds(q * m + to * cq, cq)], pg.at[z, pl.ds(q * cq, cq), pl.ds(a * rb, rb)],
-                    psend.at[q, step], precv.at[q, step], (to, z, h))
+        return send(pt.at[pl.ds((c // cq) * m + to * cq + c % cq, n)], pg.at[z, pl.ds(c, n), pl.ds(a * rb, rb)],
+                    psend.at[c, step], precv.at[c, step], (to, z, h))
 
     def w_copy(step):
         return send(w_ref, wall.at[h], wsend.at[step], wrecv.at[step], (a, z, lax.rem(h + step, nh)))
@@ -118,15 +126,17 @@
     for q in range(nq):
         if q:
             p_turn(q)
-        for step in range(1, na):
-            p_copy(q, step).start()
+        for piece in pieces(q):
+            for step in range(1, na):
+                p_copy(piece, step).start()
     for q in range(nq):
         for r in range(cq):
             pg[z, q * cq + r, pl.ds(a * rb, rb), :] = pt[q * m + a * cq + r]
 
-    def z_copy(q, block, up):
-        ref = pg.at[block, pl.ds(q * cq, cq)]
-        return send(ref, ref, zsend.at[q, block, 0 if up else 1], zrecv.at[q, block],
+    def z_copy(piece, block, up):
+        c, n = piece
+        ref = pg.at[block, pl.ds(c, n)]
+        return send(ref, ref, zsend.at[c, block, 0 if up else 1], zrecv.at[c, block],
                     (a, z + 1 if up else z - 1, h))
 
     def goes_up(q):
@@ -136,27 +146,30 @@
         return z > (0 if q < q0 else 1)
 
     def z_own(q):
-        for step in range(1, na):
-            p_copy(q, step).wait_recv()
-
-        @pl.when(goes_up(q))
-        def _():
-            z_copy(q, z, True).start()
-
-        @pl.when(goes_down(q))
-        def _():
-            z_copy(q, z, False).start()
+        for piece in pieces(q):
+            for step in range(1, na):
+                p_copy(piece, step).wait_recv()
+
+            @pl.when(goes_up(q))
+            def _(piece=piece):
+                z_copy(piece, z, True).start()
+
+            @pl.when(goes_down(q))
+            def _(piece=piece):
+                z_copy(piece, z, False).start()
 
     def z_forward(q, hop):
         @pl.when((z >= hop) & goes_up(q))
         def _():
-            z_copy(q, z - hop, True).wait_recv()
-            z_copy(q, z - hop, True).start()
+            for piece in pieces(q):
+                z_copy(piece, z - hop, True).wait_recv()
+                z_copy(piece, z - hop, True).start()
 
         @pl.when((z + hop < nz) & goes_down(q))
         def _():
-            z_copy(q, z + hop, False).wait_recv()
-            z_copy(q, z + hop, False).start()
+            for piece in pieces(q):
+                z_copy(piece, z + hop, False).wait_recv()
+                z_copy(piece, z + hop, False).start()
 
     def z_rest(q):
         for hop in range(1, nz):
@@ -164,11 +177,13 @@
 
             @pl.when((z >= hop) & jnp.logical_not(goes_up(q)) & here)
             def _(hop=hop):
-                z_copy(q, z - hop, True).wait_recv()
+                for piece in pieces(q):
+                    z_copy(piece, z - hop, True).wait_recv()
 
             @pl.when((z + hop < nz) & jnp.logical_not(goes_down(q)) & here)
             def _(hop=hop):
-                z_copy(q, z + hop, False).wait_recv()
+                for piece in pieces(q):
+                    z_copy(piece, z + hop, False).wait_recv()
 
     eye_d = eye(d)
     column = jnp.transpose(jnp.broadcast_to(gain_ref[...], (k, d)))
@@ -281,8 +296,12 @@
                     gsend.at[q, b, step], grecv.at[q, b, step], plane(g))
 
     def out_copy(b, step):
-        ref = out_ref.at[pl.ds(h * rh + b * br, br)]
-        return send(ref, ref, osend.at[b, step], orecv.at[b, step], (a, z, lax.rem(h + step, nh)))
+        return send(outv.at[pl.ds(b * br, br)], out_hbm.at[pl.ds(h * rh + b * br, br)],
+                    osend.at[b, step], orecv.at[b, step], (a, z, lax.rem(h + step, nh)))
+
+    def keep_copy(b):
+        return pltpu.make_async_copy(
+            outv.at[pl.ds(b * br, br)], out_hbm.at[pl.ds(h * rh + b * br, br)], keep.at[b])
 
     def r1_copy(q, step):
         to = lax.rem(h + step, nh)
@@ -293,34 +312,57 @@
         for step in range(1, nh):
             r1_copy(q, step).wait_recv()
             mine = mine + rx1[q, step]
-        for n in range(s.naz):
-            mine_s[n, q] = mine[n * s.rs:(n + 1) * s.rs]
-
-    def peer_n(step):
-        return lax.rem(me_n + step, s.naz)
+        for o in range(s.no):
+            mine_s[o, q] = mine[o * s.rs:(o + 1) * s.rs]
 
     def at_n(n):
         return (lax.div(n, nz), lax.rem(n, nz), h)
 
+    def owner(o):
+        return (o // s.per * s.stride, s.base + o % s.per)
+
+    def other(o):
+        return (a != owner(o)[0]) | (z != owner(o)[1])
+
+    me_o = lax.div(a, s.stride) * s.per + z - s.base
+    is_owner = (lax.rem(a, s.stride) == 0) & (z >= s.base) & (z < s.base + s.per)
     batches = [(0, nq - 1), (nq - 1, nq)] if nq > 1 else [(0, nq)]
 
-    def r2_copy(batch, step):
+    def r2_copy(batch, o, n):
         lo, hi = batches[batch]
-        n = peer_n(step)
-        return send(mine_s.at[n, lo:hi], rx2.at[step, lo:hi], r2s.at[batch, step], r2r.at[batch, step], at_n(n))
+        return send(mine_s.at[o, lo:hi], rx2.at[n, lo:hi],
+                    r2s.at[batch, o], r2r.at[batch, n], (*owner(o), h))
+
+    def r2_start(batch):
+        for o in range(s.no):
+            @pl.when(other(o))
+            def _(o=o):
+                r2_copy(batch, o, me_n).start()
+
+    def r3_copy(batch, o, step):
+        lo, hi = batches[batch]
+        ref = rx3.at[o, lo:hi]
+        return send(ref, ref, r3s.at[batch, step], r3r.at[batch, o], at_n(lax.rem(me_n + step, s.naz)))
 
     def r2_sum(batch):
         lo, hi = batches[batch]
-        mine = mine_s[me_n, lo:hi]
-        for step in range(1, s.naz):
-            r2_copy(batch, step).wait_recv()
-            mine = mine + rx2[step, lo:hi]
-        rx3[me_n, lo:hi] = mine
-
-    def r3_copy(batch, step):
-        lo, hi = batches[batch]
-        ref = rx3.at[me_n, lo:hi]
-        return send(ref, ref, r3s.at[batch, step], r3r.at[batch, step], at_n(peer_n(step)))
+
+        @pl.when(is_owner)
+        def _():
+            mine = mine_s[me_o, lo:hi]
+            for step in range(1, s.naz):
+                n = lax.rem(me_n + step, s.naz)
+                r2_copy(batch, 0, n).wait_recv()
+                mine = mine + rx2[n, lo:hi]
+            rx3[me_o, lo:hi] = mine
+            for step in range(1, s.naz):
+                r3_copy(batch, me_o, step).start()
+
+    def r3_wait(batch):
+        for o in range(s.no):
+            @pl.when(other(o))
+            def _(o=o):
+                r3_copy(batch, o, 1).wait_recv()
 
     def sq_copy(step):
         return send(sq.at[0], sq.at[step], qs.at[step], qr.at[step], (a, z, lax.rem(h + step, nh)))
@@ -367,9 +409,10 @@
             second = jnp.mean(scaled * unit, axis=0, keepdims=True)
             res = (inv_s[t] * (scaled - first - unit * second)).astype(BF16)
             for e in range(2):
-                out_ref[h * rh + 2 * t + e] = dot(eye_k, res[:, e * k:(e + 1) * k], NT).astype(BF16)
+                outv[2 * t + e] = dot(eye_k, res[:, e * k:(e + 1) * k], NT).astype(BF16)
             return carry
         lax.fori_loop(0, br // 2, one, 0, unroll=2)
+        keep_copy(b).start()
         for step in range(1, nh):
             out_copy(b, step).start()
 
@@ -436,83 +479,85 @@
             in_copy(q, inward).start()
 
     last = nq - 1
-    late = 0
-    before = []
+    queue = []
+
+    def run(count):
+        for _ in range(min(count, len(queue))):
+            q, b = queue.pop(0)
+            gather(q, b)
+            if b == nb - 1:
+                for step in range(1, nh):
+                    r1_copy(q, step).start()
+
     for q in range(nq):
         make(q)
+        if q > 1:
+            queue += [(q - 2, b) for b in range(nb)]
+        if q == last:
+            queue += [(last - 1, b) for b in range(nb)] if q else []
+            run(max(len(queue) - 2 * nb, 0))
         for b in range(nb):
+            run(1 if q < last else 0)
             came_back(q, b)
             g_send(q, b)
-            for _ in range(2):
-                if before:
-                    gather(*before.pop(0))
-            if q == last and not before and b > 1:
-                at = b - 2 - late
-                gather(last, at)
-                norm_back(at)
-            elif q == last and b > 1:
-                late += 1
-        for task in before:
-            gather(*task)
-        before = [(q, b) for b in range(nb)]
-        if q:
-            for step in range(1, nh):
-                r1_copy(q - 1, step).start()
+            if q == last:
+                run(3 if b < nb - 1 else 0)
+                if b > 0:
+                    queue.append((last, b - 1))
+    queue.append((last, nb - 1))
+    run(max(len(queue) - 1, 0))
     if nq > 1:
         for q in range(nq - 1):
             r1_sum(q)
-        for step in range(1, s.naz):
-            r2_copy(0, step).start()
-    for b in range(max(nb - 2 - late, 0), nb):
-        gather(last, b)
-        if b == nb - 1:
-            for step in range(1, nh):
-                r1_copy(last, step).start()
-            if nq > 1:
-                r2_sum(0)
-                for step in range(1, s.naz):
-                    r3_copy(0, step).start()
-        else:
-            norm_back(b)
+        r2_start(0)
+    run(1)
+    norm_back(0)
     r1_sum(last)
-    end = len(batches) - 1
-    for step in range(1, s.naz):
-        r2_copy(end, step).start()
-    norm_back(nb - 1)
-    r2_sum(end)
-    for step in range(1, s.naz):
-        r3_copy(end, step).start()
+    r2_start(len(batches) - 1)
+    waiting = list(range(len(batches)))
+    for b in range(1, nb):
+        norm_back(b)
+        if len(waiting) > 1:
+            r2_sum(waiting.pop(0))
+    for batch in waiting:
+        r2_sum(batch)
     for batch in range(len(batches)):
-        for step in range(1, s.naz):
-            r3_copy(batch, step).wait_recv()
-    found = rx3[...].reshape(s.naz * nq, s.rs, d)
-    row = jnp.sum(jnp.sum(found * found, axis=0), axis=0, keepdims=True)
-    sq[0] = jnp.broadcast_to(row, (8, d))
+        r3_wait(batch)
+    found = rx3[...].reshape(s.no * nq, s.rs, d)
+    sq[0] = jnp.sum(found * found, axis=0)
     for step in range(1, nh):
         sq_copy(step).start()
     for step in range(1, nh):
         sq_copy(step).wait()
-    squares = jnp.sum(jnp.sum(sq[...], axis=0)[0:1, :], axis=1, keepdims=True)
+    squares = jnp.sum(jnp.sum(jnp.sum(sq[...], axis=0), axis=0, keepdims=True), axis=1, keepdims=True)
     factor = jnp.minimum(1.0, CLIP_LIMIT * lax.rsqrt(squares + 1e-06))
     for q in range(nq):
-        full = jnp.concatenate([rx3[n, q] for n in range(s.naz)], axis=0) * factor
-        for w in range(4):
-            wg_ref[w, q * m:(q + 1) * m, :] = full[w * m:(w + 1) * m]
+        for o in range(s.no):
+            w, at = o * s.rs // m, q * m + o * s.rs % m
+            wg_ref[w, at:at + s.rs, :] = rx3[o, q] * factor
 
     for b in range(nb):
+        keep_copy(b).wait()
         for step in range(1, nh):
             out_copy(b, step).wait()
     for step in range(1, nh):
         w_copy(step).wait_send()
     for batch in range(len(batches)):
-        for step in range(1, s.naz):
-            r2_copy(batch, step).wait_send()
-            r3_copy(batch, step).wait_send()
+        for o in range(s.no):
+            @pl.when(other(o))
+            def _(batch=batch, o=o):
+                r2_copy(batch, o, me_n).wait_send()
+
+        @pl.when(is_owner)
+        def _(batch=batch):
+            for step in range(1, s.naz):
+                r3_copy(batch, me_o, step).wait_send()
     for q in range(nq):
         for step in range(1, nh):
             r1_copy(q, step).wait_send()
-        for step in range(1, na):
-            p_copy(q, step).wait_send()
+        for piece in pieces(q):
+            for step in range(1, na):
+                p_copy(piece, step).wait_send()
         for step in range(1, g_n):
             lr_copy(q, step).wait_send()
             for b in range(nb):
@@ -520,11 +565,13 @@
         for hop in range(nz):
             @pl.when((z >= hop) & goes_up(q))
             def _(q=q, hop=hop):
-                z_copy(q, z - hop, True).wait_send()
+                for piece in pieces(q):
+                    z_copy(piece, z - hop, True).wait_send()
 
             @pl.when((z + hop < nz) & goes_down(q))
             def _(q=q, hop=hop):
-                z_copy(q, z + hop, False).wait_send()
+                for piece in pieces(q):
+                    z_copy(piece, z + hop, False).wait_send()
         if q >= q0:
             @pl.when(is_end)
             def _(q=q):
@@ -543,7 +590,6 @@
     vm = pl.BlockSpec(memory_space=pltpu.VMEM)
     dma = pltpu.SemaphoreType.DMA
     half = s.rh // 2
-    slices = (s.naz, s.nq, s.rs, depth)
     scratch = [
         pltpu.VMEM((s.rh, cols, depth), BF16),
         pltpu.VMEM((ch, rows, cols), BF16),
@@ -565,18 +611,19 @@
         pltpu.VMEM((2, s.hid, s.rh, cols), BF16),
         pltpu.VMEM((2, s.nc * s.tp, cols), F32),
         pltpu.VMEM((half, depth, 2 * cols), F32),
+        pltpu.VMEM((s.rh, cols, depth), BF16),
         pltpu.VMEM((s.nq, nh, 4 * s.m, depth), F32),
         pltpu.VMEM((s.nq, nh, 4 * s.m, depth), F32),
-        pltpu.VMEM(slices, F32),
-        pltpu.VMEM(slices, F32),
-        pltpu.VMEM(slices, F32),
-        pltpu.VMEM((nh, 8, depth), F32),
+        pltpu.VMEM((s.no, s.nq, s.rs, depth), F32),
+        pltpu.VMEM((s.naz, s.nq, s.rs, depth), F32),
+        pltpu.VMEM((s.no, s.nq, s.rs, depth), F32),
+        pltpu.VMEM((nh, s.rs, depth), F32),
         dma(()), dma((nh,)), dma((nh,)),
-        dma((s.nq, na)), dma((s.nq, na)), dma((s.nq, nz, 2)), dma((s.nq, nz)),
+        dma((s.cp, na)), dma((s.cp, na)), dma((s.cp, nz, 2)), dma((s.cp, nz)),
         dma((s.nq, s.g)), dma((s.nq, s.g)), dma((s.nq, s.nb, s.g)), dma((s.nq, s.nb, s.g)),
         dma((s.nb, nh)), dma((s.nb, nh)),
-        dma((s.nq, nh)), dma((s.nq, nh)), dma((2, s.naz)), dma((2, s.naz)), dma((2, s.naz)), dma((2, s.naz)),
-        dma((nh,)), dma((nh,)),
+        dma((s.nq, nh)), dma((s.nq, nh)), dma((2, s.no)), dma((2, s.naz)), dma((2, s.naz)), dma((2, s.no)),
+        dma((nh,)), dma((nh,)), dma((s.nb,)),
         dma((s.helped,)), dma((s.helped,)), dma((s.helped, s.nb)), dma((s.helped, s.nb)),
     ]
     pair_grad, found = pl.pallas_call(
@@ -586,7 +633,7 @@
             jax.ShapeDtypeStruct((4, ch, depth), F32),
         ),
         in_specs=[vm, pl.BlockSpec(memory_space=pl.ANY), vm, vm, vm, pl.BlockSpec(memory_space=pltpu.SMEM)],
-        out_specs=(vm, vm),
+        out_specs=(pl.BlockSpec(memory_space=pl.ANY), vm),
         scratch_shapes=scratch,
         compiler_params=pltpu.CompilerParams(
             collective_id=0, has_side_effects=True, vmem_limit_bytes=VMEM_LIMIT),

time: 173 us -> 162 us (0.936)
  Pallas kernels: 167 us -> 156 us
    pallas_call x1, Pallas kernels: 167 us -> 156 us  [on_device(): pl.pallas_call(functools.partial(kernel, s), out_shape=(jax.ShapeDtypeStr...]
where the time goes in v3:
time: 162 us
  Pallas kernels  156 us (96%)
  local copies, waits for them, and re-layouts  5.48 us (3%)
    pallas_call x1, Pallas kernels, on_device(): pl.pallas_call(functools.partial(kernel, s), out_shape=(jax.ShapeDtypeStr...  156 us
    unnamed x4, local copies, waits for them, and re-layouts  5.48 us

profile of v3, /device:TPU:0, one launch (start us, length us, event | category | flops | bytes accessed | tf_op | source)
XLA Modules:
  0.0 161.9 jit_solution(10574375211017382541)
XLA Ops:
  0.6 155.7 %shard_map.68 = (bf16[128,128,128]{2,1,0:T(8,128)(2,1)}, f32[4,64,128]{2,1,0:T(8,128)}) custom-call(bf16[128,64,128]{2,1,0:T(8,128)(2,1)} %p_ref.1, bf16[128,128,128]{2,1,0:T(8,128)(2,1)} %x_hbm.1, bf16[4,64,128]{2,1,0:T(8,128)(2,1)} %bitcast.5, f32[1,128]{1,0:T(1,128)} %bitcast.7, s32[4,128]{1,0:T(4,128)} %bitcast.6, s32[512]{0:T(512)} %mask_s.1), custom_call_target="tpu_custom_call" | custom-call | tf_op jit(solution)/shard_map/pallas_call | solution.py:629
  156.4 0.0 copy-start
  156.4 4.8 %copy.9 = bf16[128,128,128]{2,1,0:T(8,128)(2,1)} copy(bf16[128,128,128]{2,1,0:T(8,128)(2,1)} %get-tuple-element.8) | data formatting | bytes 8388608
  161.2 0.0 copy-done
  161.2 0.7 copy.10
Async XLA Ops:
  156.4 4.8 %copy-start = (f32[4,64,128]{2,1,0:T(8,128)S(1)}, f32[4,64,128]{2,1,0:T(8,128)}, u32[]{:S(2)}) copy-start(f32[4,64,128]{2,1,0:T(8,128)} %get-tuple-element.5) | copy-start | bytes 393220

commit v4 on v3

--- a/solution.py
+++ b/solution.py
@@ -59,7 +59,7 @@
         self.helped = max(self.nq - self.q0, 1)
 
 
-def kernel(s, p_ref, x_hbm, w_ref, gain_ref, mask_ref, mask_s, out_hbm, wg_ref,
+def kernel(s, p_ref, x_hbm, w_ref, gain_ref, mask_ref, mask_s, out_hbm, wg_ref, sq_ref,
            xv, pt, pg, wall, wt, gain, unit_s, inv_s, nt_s, pr, fac, relay, lrs, lrb, lrh, gs, gsh, gr, turn, ng,
            outv, raw, rx1, mine_s, rx2, rx3, sq,
            xsem, wsend, wrecv, psend, precv, zsend, zrecv, lsend, lrecv, gsend, grecv, osend, orecv,
@@ -82,6 +82,9 @@
     def peer_g(step):
         return lax.rem(me_g + step, g_n)
 
+    def sent(ref, sem):
+        pltpu.make_async_copy(ref, ref, sem).wait()
+
     def send(src, dst, send_sem, recv_sem, device):
         return pltpu.make_async_remote_copy(
             src_ref=src, dst_ref=dst, send_sem=send_sem, recv_sem=recv_sem,
@@ -114,7 +117,7 @@
         c, n = piece
         to = lax.rem(a + step, na)
         return send(pt.at[pl.ds((c // cq) * m + to * cq + c % cq, n)], pg.at[z, pl.ds(c, n), pl.ds(a * rb, rb)],
-                    psend.at[c, step], precv.at[c, step], (to, z, h))
+                    psend, precv.at[c, step], (to, z, h))
 
     def w_copy(step):
         return send(w_ref, wall.at[h], wsend.at[step], wrecv.at[step], (a, z, lax.rem(h + step, nh)))
@@ -136,7 +139,7 @@
     def z_copy(piece, block, up):
         c, n = piece
         ref = pg.at[block, pl.ds(c, n)]
-        return send(ref, ref, zsend.at[c, block, 0 if up else 1], zrecv.at[c, block],
+        return send(ref, ref, zsend.at[c // cq, 0 if up else 1], zrecv.at[c, block],
                     (a, z + 1 if up else z - 1, h))
 
     def goes_up(q):
@@ -145,8 +148,8 @@
     def goes_down(q):
         return z > (0 if q < q0 else 1)
 
-    def z_own(q):
-        for piece in pieces(q):
+    def z_own(q, some=None):
+        for piece in some or pieces(q):
             for step in range(1, na):
                 p_copy(piece, step).wait_recv()
 
@@ -231,7 +234,17 @@
         def one(sub, carry, b=b):
             rows_step(b * (br // 2) + sub, sub)
             return carry
-        lax.fori_loop(0, br // 2, one, 0)
+        parts = pieces(0) if b == 0 else [None]
+        each = br // 2 // len(parts)
+        if each * len(parts) * 2 == br:
+            for n, piece in enumerate(parts):
+                lax.fori_loop(n * each, (n + 1) * each, one, 0)
+                if piece:
+                    z_own(0, [piece])
+        else:
+            lax.fori_loop(0, br // 2, one, 0)
+            if b == 0:
+                z_own(0)
 
         def flush(c, carry, b=b):
             for side in range(2):
@@ -239,7 +252,7 @@
                 lrs[side, c, b * br:(b + 1) * br, :] = tile.astype(BF16)
             return carry
         lax.fori_loop(0, hid, flush, 0, unroll=4)
-        if b < q0:
+        if 0 < b < q0:
             z_own(b)
     for q in range(nb, q0):
         z_own(q)
@@ -252,7 +265,7 @@
     def lr_copy(q, step):
         return send(lrs.at[:, pl.ds(q * nc + peer_g(step) * cq, cq)],
                     lrb.at[:, pl.ds(q * cq, cq), pl.ds(row0, rh)],
-                    lsend.at[q, step], lrecv.at[q, step], plane(peer_g(step)))
+                    lsend, lrecv.at[q, step], plane(peer_g(step)))
 
     for q in [*range(q0, nq), *range(q0)]:
         for step in range(1, g_n):
@@ -281,19 +294,19 @@
 
     def in_copy(q, z_to):
         return send(lrb.at[:, pl.ds(q * cq, cq)], lrh.at[:, pl.ds((q - q0) * cq, cq)],
-                    hls.at[q - q0], hlr.at[q - q0], (a, z_to, h))
+                    hls, hlr.at[q - q0], (a, z_to, h))
 
     def back_copy(q, b, z_to):
         return send(gsh.at[:, pl.ds((q - q0) * cq, cq), :, pl.ds(b * br, br)],
                     gs.at[:, pl.ds(q * cq, cq), :, pl.ds(b * br, br)],
-                    hgs.at[q - q0, b], hgr.at[q - q0, b], (a, z_to, h))
+                    hgs, hgr.at[q - q0, b], (a, z_to, h))
 
     def g_copy(q, b, step):
         g = peer_g(step)
         place = lax.rem(g, na) * nh + lax.div(g, na)
         return send(gs.at[:, pl.ds(q * cq, cq), place, pl.ds(b * br, br)],
                     gr.at[:, pl.ds(q * nc + me_g * cq, cq), pl.ds(b * br, br)],
-                    gsend.at[q, b, step], grecv.at[q, b, step], plane(g))
+                    gsend.at[q], grecv.at[q, b, step], plane(g))
 
     def out_copy(b, step):
         return send(outv.at[pl.ds(b * br, br)], out_hbm.at[pl.ds(h * rh + b * br, br)],
@@ -331,7 +344,7 @@
     def r2_copy(batch, o, n):
         lo, hi = batches[batch]
         return send(mine_s.at[o, lo:hi], rx2.at[n, lo:hi],
-                    r2s.at[batch, o], r2r.at[batch, n], (*owner(o), h))
+                    r2s.at[batch], r2r.at[batch, n], (*owner(o), h))
 
     def r2_start(batch):
         for o in range(s.no):
@@ -342,7 +355,7 @@
     def r3_copy(batch, o, step):
         lo, hi = batches[batch]
         ref = rx3.at[o, lo:hi]
-        return send(ref, ref, r3s.at[batch, step], r3r.at[batch, o], at_n(lax.rem(me_n + step, s.naz)))
+        return send(ref, ref, r3s.at[batch], r3r.at[batch, o], at_n(lax.rem(me_n + step, s.naz)))
 
     def r2_sum(batch):
         lo, hi = batches[batch]
@@ -477,6 +490,32 @@
         for q in range(q0, nq):
             lr_wait(q)
             in_copy(q, inward).start()
+
+    def drain():
+        for step in range(1, nh):
+            w_copy(step).wait_send()
+        sent(pt.at[pl.ds(0, (na - 1) * s.cp)], psend)
+        sent(lrs.at[:, pl.ds(0, (g_n - 1) * nq * cq)], lsend)
+        for q in range(nq):
+            for step in range(1, nh):
+                r1_copy(q, step).wait_send()
+            sent(gs.at[:, pl.ds(q * cq, cq), pl.ds(0, g_n - 1)], gsend.at[q])
+            for count in range(1, nz):
+                @pl.when((z + 1 == count) & goes_up(q))
+                def _(q=q, count=count):
+                    sent(pg.at[pl.ds(0, count), pl.ds(q * cq, cq)], zsend.at[q, 0])
+
+                @pl.when((nz - z == count) & goes_down(q))
+                def _(q=q, count=count):
+                    sent(pg.at[pl.ds(0, count), pl.ds(q * cq, cq)], zsend.at[q, 1])
+        if q0 < nq:
+            @pl.when(is_end)
+            def _():
+                sent(lrh, hls)
+
+            @pl.when(is_near)
+            def _():
+                sent(gsh, hgs)
 
     last = nq - 1
     queue = []
@@ -521,6 +560,7 @@
             r2_sum(waiting.pop(0))
     for batch in waiting:
         r2_sum(batch)
+    drain()
     for batch in range(len(batches)):
         r3_wait(batch)
     found = rx3[...].reshape(s.no * nq, s.rs, d)
@@ -529,58 +569,48 @@
         sq_copy(step).start()
     for step in range(1, nh):
         sq_copy(step).wait()
-    squares = jnp.sum(jnp.sum(jnp.sum(sq[...], axis=0), axis=0, keepdims=True), axis=1, keepdims=True)
-    factor = jnp.minimum(1.0, CLIP_LIMIT * lax.rsqrt(squares + 1e-06))
+    sq_ref[...] = jnp.sum(sq[...], axis=0)
     for q in range(nq):
         for o in range(s.no):
             w, at = o * s.rs // m, q * m + o * s.rs % m
-            wg_ref[w, at:at + s.rs, :] = rx3[o, q] * factor
+            wg_ref[w, at:at + s.rs, :] = rx3[o, q]
 
     for b in range(nb):
         keep_copy(b).wait()
         for step in range(1, nh):
             out_copy(b, step).wait()
-    for step in range(1, nh):
-        w_copy(step).wait_send()
-    for batch in range(len(batches)):
-        for o in range(s.no):
-            @pl.when(other(o))
-            def _(batch=batch, o=o):
-                r2_copy(batch, o, me_n).wait_send()
-
+    for batch, (lo, hi) in enumerate(batches):
         @pl.when(is_owner)
-        def _(batch=batch):
-            for step in range(1, s.naz):
-                r3_copy(batch, me_o, step).wait_send()
-    for q in range(nq):
-        for step in range(1, nh):
-            r1_copy(q, step).wait_send()
-        for piece in pieces(q):
-            for step in range(1, na):
-                p_copy(piece, step).wait_send()
-        for step in range(1, g_n):
-            lr_copy(q, step).wait_send()
-            for b in range(nb):
-                g_copy(q, b, step).wait_send()
-        for hop in range(nz):
-            @pl.when((z >= hop) & goes_up(q))
-            def _(q=q, hop=hop):
-                for piece in pieces(q):
-                    z_copy(piece, z - hop, True).wait_send()
-
-            @pl.when((z + hop < nz) & goes_down(q))
-            def _(q=q, hop=hop):
-                for piece in pieces(q):
-                    z_copy(piece, z + hop, False).wait_send()
-        if q >= q0:
-            @pl.when(is_end)
-            def _(q=q):
-                in_copy(q, inward).wait_send()
-
-            @pl.when(is_near)
-            def _(q=q):
-                for b in range(nb):
-                    back_copy(q, b, outward).wait_send()
+        def _(batch=batch, lo=lo, hi=hi):
+            sent(mine_s.at[pl.ds(0, s.no - 1), lo:hi], r2s.at[batch])
+            sent(rx2.at[pl.ds(0, s.naz - 1), lo:hi], r3s.at[batch])
+
+        @pl.when(jnp.logical_not(is_owner))
+        def _(batch=batch, lo=lo, hi=hi):
+            sent(mine_s.at[:, lo:hi], r2s.at[batch])
+
+
+def finish(blocks, from_hbm, found_ref, sq_ref, out_hbm, wg_ref, held, sem_in, sem_out):
+    size = held.shape[0] // blocks
+
+    def came(b):
+        at = pl.ds(b * size, size)
+        return pltpu.make_async_copy(from_hbm.at[at], held.at[at], sem_in.at[b])
+
+    def leaves(b):
+        at = pl.ds(b * size, size)
+        return pltpu.make_async_copy(held.at[at], out_hbm.at[at], sem_out.at[b])
+
+    for b in range(blocks):
+        came(b).start()
+    squares = jnp.sum(jnp.sum(sq_ref[...], axis=0, keepdims=True), axis=1, keepdims=True)
+    factor = jnp.minimum(1.0, CLIP_LIMIT * lax.rsqrt(squares + 1e-06))
+    wg_ref[...] = found_ref[...] * factor
+    for b in range(blocks):
+        came(b).wait()
+        leaves(b).start()
+    for b in range(blocks):
+        leaves(b).wait()
 
 
 def on_device(na, nz, nh, pair_rep, norm_gain, weights, residue_mask, product_grad):
@@ -619,27 +649,39 @@
         pltpu.VMEM((s.no, s.nq, s.rs, depth), F32),
         pltpu.VMEM((nh, s.rs, depth), F32),
         dma(()), dma((nh,)), dma((nh,)),
-        dma((s.cp, na)), dma((s.cp, na)), dma((s.cp, nz, 2)), dma((s.cp, nz)),
-        dma((s.nq, s.g)), dma((s.nq, s.g)), dma((s.nq, s.nb, s.g)), dma((s.nq, s.nb, s.g)),
+        dma(()), dma((s.cp, na)), dma((s.nq, 2)), dma((s.cp, nz)),
+        dma(()), dma((s.nq, s.g)), dma((s.nq,)), dma((s.nq, s.nb, s.g)),
         dma((s.nb, nh)), dma((s.nb, nh)),
-        dma((s.nq, nh)), dma((s.nq, nh)), dma((2, s.no)), dma((2, s.naz)), dma((2, s.naz)), dma((2, s.no)),
+        dma((s.nq, nh)), dma((s.nq, nh)), dma((2,)), dma((2, s.naz)), dma((2,)), dma((2, s.no)),
         dma((nh,)), dma((nh,)), dma((s.nb,)),
-        dma((s.helped,)), dma((s.helped,)), dma((s.helped, s.nb)), dma((s.helped, s.nb)),
+        dma(()), dma((s.helped,)), dma(()), dma((s.helped, s.nb)),
     ]
-    pair_grad, found = pl.pallas_call(
+    grad, found, squares = pl.pallas_call(
         functools.partial(kernel, s),
         out_shape=(
             jax.ShapeDtypeStruct((rows, cols, depth), BF16),
             jax.ShapeDtypeStruct((4, ch, depth), F32),
+            jax.ShapeDtypeStruct((s.rs, depth), F32),
         ),
         in_specs=[vm, pl.BlockSpec(memory_space=pl.ANY), vm, vm, vm, pl.BlockSpec(memory_space=pltpu.SMEM)],
-        out_specs=(pl.BlockSpec(memory_space=pl.ANY), vm),
+        out_specs=(pl.BlockSpec(memory_space=pl.ANY), vm, vm),
         scratch_shapes=scratch,
         compiler_params=pltpu.CompilerParams(
             collective_id=0, has_side_effects=True, vmem_limit_bytes=VMEM_LIMIT),
     )(product_grad, pair_rep, weights.transpose(0, 2, 1), norm_gain.reshape(1, depth),
       residue_mask.reshape(nz, cols), residue_mask)
-    return (pair_grad, found.transpose(0, 2, 1))
+    blocks = math.gcd(rows, 8)
+    pair_grad, weight_grads = pl.pallas_call(
+        functools.partial(finish, blocks),
+        out_shape=(
+            jax.ShapeDtypeStruct((rows, cols, depth), BF16),
+            jax.ShapeDtypeStruct((4, ch, depth), F32),
+        ),
+        in_specs=[pl.BlockSpec(memory_space=pl.ANY), vm, vm],
+        out_specs=(pl.BlockSpec(memory_space=pl.ANY), vm),
+        scratch_shapes=[pltpu.VMEM((rows, cols, depth), BF16), dma((blocks,)), dma((blocks,))],
+    )(grad, found, squares)
+    return (pair_grad, weight_grads.transpose(0, 2, 1))
 
 
 def solution(mesh):

time: 162 us -> 157 us (0.969)
  local copies, waits for them, and re-layouts: 5.48 us -> 0 us
    unnamed x4 -> x0, local copies, waits for them, and re-layouts: 5.48 us -> none
    pallas_call x0 -> x1, Pallas kernels: none -> 5.14 us  [on_device(): pl.pallas_call(functools.partial(finish, blocks), out_shape=(jax.ShapeDty...]
    pallas_call x1, Pallas kernels: 156 us -> 151 us  [on_device(): pl.pallas_call(functools.partial(kernel, s), out_shape=(jax.ShapeDtypeStr...]
where the time goes in v4:
time: 157 us
  Pallas kernels  156 us (99%)
    pallas_call x1, Pallas kernels, on_device(): pl.pallas_call(functools.partial(kernel, s), out_shape=(jax.ShapeDtypeStr...  151 us
    pallas_call x1, Pallas kernels, on_device(): pl.pallas_call(functools.partial(finish, blocks), out_shape=(jax.ShapeDty...  5.14 us

profile of v4, /device:TPU:0, one launch (start us, length us, event | category | flops | bytes accessed | tf_op | source)
XLA Modules:
  0.0 156.6 jit_solution(9979892699462442019)
XLA Ops:
  0.6 150.8 %shard_map.68 = (bf16[128,128,128]{2,1,0:T(8,128)(2,1)}, f32[4,64,128]{2,1,0:T(8,128)}, f32[8,128]{1,0:T(8,128)}) custom-call(bf16[128,64,128]{2,1,0:T(8,128)(2,1)} %p_ref.1, bf16[128,128,128]{2,1,0:T(8,128)(2,1)} %x_hbm.1, bf16[4,64,128]{2,1,0:T(8,128)(2,1)} %bitcast.4, f32[1,128]{1,0:T(1,128)} %bitcast.6, s32[4,128]{1,0:T(4,128)} %bitcast.5, s32[512]{0:T(512)} %mask_s.1), custom_call_target="tpu_custom_call" | custom-call | tf_op jit(solution)/shard_map/pallas_call | solution.py:659
  151.5 5.1 %shard_map.69 = (bf16[128,128,128]{2,1,0:T(8,128)(2,1)}, f32[4,64,128]{2,1,0:T(8,128)}) custom-call(bf16[128,128,128]{2,1,0:T(8,128)(2,1)} %get-tuple-element.7.from_hbm, f32[4,64,128]{2,1,0:T(8,128)} %get-tuple-element.8.found_ref, f32[8,128]{1,0:T(8,128)} %get-tuple-element.9.sq_ref), custom_call_target="tpu_custom_call" | custom-call | tf_op jit(solution)/shard_map/pallas_call | solution.py:674

commit v5 on v4

--- a/solution.py
+++ b/solution.py
@@ -59,11 +59,11 @@
         self.helped = max(self.nq - self.q0, 1)
 
 
-def kernel(s, p_ref, x_hbm, w_ref, gain_ref, mask_ref, mask_s, out_hbm, wg_ref, sq_ref,
-           xv, pt, pg, wall, wt, gain, unit_s, inv_s, nt_s, pr, fac, relay, lrs, lrb, lrh, gs, gsh, gr, turn, ng,
-           outv, raw, rx1, mine_s, rx2, rx3, sq,
-           xsem, wsend, wrecv, psend, precv, zsend, zrecv, lsend, lrecv, gsend, grecv, osend, orecv,
-           r1s, r1r, r2s, r2r, r3s, r3r, qs, qr, keep, hls, hlr, hgs, hgr):
+def kernel(s, p_hbm, x_hbm, w_ref, gain_ref, mask_ref, mask_s, out_hbm, found_hbm, sq_hbm,
+           xv, p_ref, pt, pg, wall, wt, gain, unit_s, inv_s, nt_s, pr, fac, relay, lrs, lrb, lrh, gs, gsh, gr, turn, ng,
+           outv, raw, rx2, rx3, sq,
+           xsem, pin, wsend, wrecv, psend, precv, zsend, zrecv, lsend, lrecv, gsend, grecv, osend, orecv,
+           r2s, r2r, r3s, r3r, qs, qr, keep, leave, hls, hlr, hgs, hgr):
     na, nz, nh, g_n, nq, cq, nc = s.na, s.nz, s.nh, s.g, s.nq, s.cq, s.nc
     rb, rh, k, d, ch, hid, br, nb, m = s.rb, s.rh, s.k, s.d, s.ch, s.hid, s.br, s.nb, s.m
     a, z, h = lax.axis_index("ia"), lax.axis_index("ja"), lax.axis_index("col")
@@ -92,14 +92,25 @@
 
     barrier = pltpu.get_barrier_semaphore()
     total = s.naz * nh
+    me_t = me_n * nh + h
+
+    def at_t(t):
+        return (lax.div(t, nz * nh), lax.rem(lax.div(t, nh), nz), lax.rem(t, nh))
+
+    def p_in(q):
+        at = pl.ds(q * m, m)
+        return pltpu.make_async_copy(p_hbm.at[:, at], p_ref.at[:, at], pin.at[q])
+
+    for q in range(nq):
+        p_in(q).start()
     for step in range(1, total):
-        to = lax.rem(me_n * nh + h + step, total)
-        device = (lax.div(to, nz * nh), lax.rem(lax.div(to, nh), nz), lax.rem(to, nh))
-        pl.semaphore_signal(barrier, inc=1, device_id=device, device_id_type=MESH)
+        pl.semaphore_signal(barrier, inc=1, device_id=at_t(lax.rem(me_t + step, total)), device_id_type=MESH)
     xcopy = pltpu.make_async_copy(x_hbm.at[pl.ds(h * rh, rh)], xv, xsem)
     xcopy.start()
 
     def p_turn(q):
+        p_in(q).wait()
+
         def block(ib, carry):
             slot = lax.rem(ib, 2)
             for ii in range(s.bi):
@@ -296,17 +307,25 @@
         return send(lrb.at[:, pl.ds(q * cq, cq)], lrh.at[:, pl.ds((q - q0) * cq, cq)],
                     hls, hlr.at[q - q0], (a, z_to, h))
 
-    def back_copy(q, b, z_to):
-        return send(gsh.at[:, pl.ds((q - q0) * cq, cq), :, pl.ds(b * br, br)],
-                    gs.at[:, pl.ds(q * cq, cq), :, pl.ds(b * br, br)],
-                    hgs, hgr.at[q - q0, b], (a, z_to, h))
-
-    def g_copy(q, b, step):
+    def cuts(q):
+        whole = [(b, 0, cq) for b in range(nb)]
+        if q == nq - 1 and q >= q0 and cq % 2 == 0:
+            return whole[:-1] + [(nb - 1, 0, cq // 2), (nb - 1, cq // 2, cq // 2)]
+        return whole
+
+    def back_copy(q, at, z_to):
+        b, lo, n = cuts(q)[at]
+        return send(gsh.at[:, pl.ds((q - q0) * cq + lo, n), :, pl.ds(b * br, br)],
+                    gs.at[:, pl.ds(q * cq + lo, n), :, pl.ds(b * br, br)],
+                    hgs, hgr.at[q - q0, at], (a, z_to, h))
+
+    def g_copy(q, at, step):
+        b, lo, n = cuts(q)[at]
         g = peer_g(step)
         place = lax.rem(g, na) * nh + lax.div(g, na)
-        return send(gs.at[:, pl.ds(q * cq, cq), place, pl.ds(b * br, br)],
-                    gr.at[:, pl.ds(q * nc + me_g * cq, cq), pl.ds(b * br, br)],
-                    gsend.at[q], grecv.at[q, b, step], plane(g))
+        return send(gs.at[:, pl.ds(q * cq + lo, n), place, pl.ds(b * br, br)],
+                    gr.at[:, pl.ds(q * nc + me_g * cq + lo, n), pl.ds(b * br, br)],
+                    gsend.at[q], grecv.at[q, at, step], plane(g))
 
     def out_copy(b, step):
         return send(outv.at[pl.ds(b * br, br)], out_hbm.at[pl.ds(h * rh + b * br, br)],
@@ -316,60 +335,60 @@
         return pltpu.make_async_copy(
             outv.at[pl.ds(b * br, br)], out_hbm.at[pl.ds(h * rh + b * br, br)], keep.at[b])
 
-    def r1_copy(q, step):
-        to = lax.rem(h + step, nh)
-        return send(raw.at[q, to], rx1.at[q, step], r1s.at[q, step], r1r.at[q, step], (a, z, to))
-
-    def r1_sum(q):
-        mine = raw[q, h]
-        for step in range(1, nh):
-            r1_copy(q, step).wait_recv()
-            mine = mine + rx1[q, step]
-        for o in range(s.no):
-            mine_s[o, q] = mine[o * s.rs:(o + 1) * s.rs]
-
     def at_n(n):
         return (lax.div(n, nz), lax.rem(n, nz), h)
 
     def owner(o):
         return (o // s.per * s.stride, s.base + o % s.per)
 
-    def other(o):
-        return (a != owner(o)[0]) | (z != owner(o)[1])
+    def other(o, half=None):
+        away = (a != owner(o)[0]) | (z != owner(o)[1])
+        return away if half is None else away | (h != half)
 
     me_o = lax.div(a, s.stride) * s.per + z - s.base
     is_owner = (lax.rem(a, s.stride) == 0) & (z >= s.base) & (z < s.base + s.per)
     batches = [(0, nq - 1), (nq - 1, nq)] if nq > 1 else [(0, nq)]
-
-    def r2_copy(batch, o, n):
+    final = len(batches) - 1
+
+    def r2_copy(batch, half, o, sender):
         lo, hi = batches[batch]
-        return send(mine_s.at[o, lo:hi], rx2.at[n, lo:hi],
-                    r2s.at[batch], r2r.at[batch, n], (*owner(o), h))
+        return send(raw.at[lo:hi, half, o], rx2.at[sender, lo:hi],
+                    r2s.at[batch], r2r.at[batch, sender], (*owner(o), half))
 
     def r2_start(batch):
-        for o in range(s.no):
-            @pl.when(other(o))
-            def _(o=o):
-                r2_copy(batch, o, me_n).start()
+        for half in range(nh):
+            for o in range(s.no):
+                @pl.when(other(o, half))
+                def _(half=half, o=o):
+                    r2_copy(batch, half, o, me_t).start()
 
     def r3_copy(batch, o, step):
         lo, hi = batches[batch]
         ref = rx3.at[o, lo:hi]
         return send(ref, ref, r3s.at[batch], r3r.at[batch, o], at_n(lax.rem(me_n + step, s.naz)))
 
+    def sq_copy(slot, step):
+        ref = sq.at[slot]
+        return send(ref, ref, qs, qr.at[slot], at_t(lax.rem(me_t + step, total)))
+
     def r2_sum(batch):
         lo, hi = batches[batch]
 
         @pl.when(is_owner)
         def _():
-            mine = mine_s[me_o, lo:hi]
-            for step in range(1, s.naz):
-                n = lax.rem(me_n + step, s.naz)
-                r2_copy(batch, 0, n).wait_recv()
-                mine = mine + rx2[n, lo:hi]
-            rx3[me_o, lo:hi] = mine
+            def one(step, mine):
+                n = lax.rem(me_t + step, total)
+                r2_copy(batch, 0, 0, n).wait_recv()
+                return mine + rx2[n, lo:hi]
+            rx3[me_o, lo:hi] = lax.fori_loop(1, total, one, raw[lo:hi, h, me_o])
             for step in range(1, s.naz):
                 r3_copy(batch, me_o, step).start()
+            if batch == final:
+                slot = h * s.no + me_o
+                found = rx3[me_o].reshape(nq * s.rs, d)
+                sq[slot] = jnp.sum(found * found, axis=0, keepdims=True)
+                for step in range(1, total):
+                    sq_copy(slot, step).start()
 
     def r3_wait(batch):
         for o in range(s.no):
@@ -377,12 +396,17 @@
             def _(o=o):
                 r3_copy(batch, o, 1).wait_recv()
 
-    def sq_copy(step):
-        return send(sq.at[0], sq.at[step], qs.at[step], qr.at[step], (a, z, lax.rem(h + step, nh)))
+    def sq_wait():
+        for half in range(nh):
+            for o in range(s.no):
+                @pl.when(other(o, half))
+                def _(slot=half * s.no + o):
+                    sq_copy(slot, 1).wait_recv()
 
     def gather(q, b):
-        for step in range(1, g_n):
-            g_copy(q, b, step).wait_recv()
+        for at, cut in enumerate(cuts(q)):
+            for step in range(1, g_n if cut[0] == b else 1):
+                g_copy(q, at, step).wait_recv()
 
         def spread(n, carry):
             for side in range(2):
@@ -391,7 +415,7 @@
             return carry
         lax.fori_loop(0, nc, spread, 0, unroll=4)
         if b == 0:
-            raw[q] = jnp.zeros((nh, 4 * m, d), F32)
+            raw[q] = jnp.zeros((nh, s.no, s.rs, d), F32)
 
         def one(sub, carry):
             t0 = b * (br // 2) + sub * s.tb
@@ -405,7 +429,7 @@
             grads = jnp.concatenate(
                 [term[half * m:(half + 1) * m] for half in range(nh) for term in terms], axis=0)
             normed = jnp.concatenate([nt_s[t0 + u] for u in range(s.tb)], axis=1)
-            raw[q] += dot(grads, normed, NT).reshape(nh, 4 * m, d)
+            raw[q] += dot(grads, normed, NT).reshape(nh, s.no, s.rs, d)
             part = dot(wt[q], grads, NN)
             for u in range(s.tb):
                 piece = part[:, u * 2 * k:(u + 1) * 2 * k]
@@ -433,11 +457,12 @@
         for step in range(1, g_n):
             lr_copy(q, step).wait_recv()
 
-    def g_send(q, b):
+    def g_send(q, at):
+        b, lo, n = cuts(q)[at]
         for step in range(1, g_n):
-            g_copy(q, b, step).start()
+            g_copy(q, at, step).start()
         for side in range(2):
-            for r in range(cq):
+            for r in range(lo, lo + n):
                 gr[side, q * nc + me_g * cq + r, b * br:(b + 1) * br, :] = gs[
                     side, q * cq + r, a * nh + h, b * br:(b + 1) * br, :]
 
@@ -453,8 +478,8 @@
             z_rest(q)
             in_copy(q, outward).wait_recv()
             triangles(q, lrh, gsh, q0)
-            for b in range(nb):
-                back_copy(q, b, outward).start()
+            for at in range(len(cuts(q))):
+                back_copy(q, at, outward).start()
             lr_wait(q)
             triangles(q, lrb, gs, 0)
 
@@ -464,11 +489,11 @@
             lr_wait(q)
             triangles(q, lrb, gs, 0)
 
-    def came_back(q, b):
+    def came_back(q, at):
         if q >= q0:
             @pl.when(is_end)
             def _():
-                back_copy(q, b, outward).wait_recv()
+                back_copy(q, at, outward).wait_recv()
 
     for hop in range(1, nz - 1):
         for q in range(q0):
@@ -497,8 +522,6 @@
         sent(pt.at[pl.ds(0, (na - 1) * s.cp)], psend)
         sent(lrs.at[:, pl.ds(0, (g_n - 1) * nq * cq)], lsend)
         for q in range(nq):
-            for step in range(1, nh):
-                r1_copy(q, step).wait_send()
             sent(gs.at[:, pl.ds(q * cq, cq), pl.ds(0, g_n - 1)], gsend.at[q])
             for count in range(1, nz):
                 @pl.when((z + 1 == count) & goes_up(q))
@@ -524,9 +547,10 @@
         for _ in range(min(count, len(queue))):
             q, b = queue.pop(0)
             gather(q, b)
-            if b == nb - 1:
-                for step in range(1, nh):
-                    r1_copy(q, step).start()
+            if b == nb - 1 and q == last - 1:
+                r2_start(0)
+            if b == nb - 1 and q == last:
+                r2_start(final)
 
     for q in range(nq):
         make(q)
@@ -535,46 +559,35 @@
         if q == last:
             queue += [(last - 1, b) for b in range(nb)] if q else []
             run(max(len(queue) - 2 * nb, 0))
-        for b in range(nb):
+        ways = cuts(q)
+        for at, (b, lo, n) in enumerate(ways):
             run(1 if q < last else 0)
-            came_back(q, b)
-            g_send(q, b)
+            came_back(q, at)
+            g_send(q, at)
             if q == last:
-                run(3 if b < nb - 1 else 0)
-                if b > 0:
+                run(3 if b < nb - 1 else 1 if at < len(ways) - 1 else 0)
+                if b and not lo:
                     queue.append((last, b - 1))
     queue.append((last, nb - 1))
     run(max(len(queue) - 1, 0))
-    if nq > 1:
-        for q in range(nq - 1):
-            r1_sum(q)
-        r2_start(0)
+    if nb > 1:
+        norm_back(0)
     run(1)
-    norm_back(0)
-    r1_sum(last)
-    r2_start(len(batches) - 1)
     waiting = list(range(len(batches)))
-    for b in range(1, nb):
-        norm_back(b)
+    for b in range(1 if nb > 1 else 0, nb):
         if len(waiting) > 1:
             r2_sum(waiting.pop(0))
+        norm_back(b)
     for batch in waiting:
         r2_sum(batch)
     drain()
     for batch in range(len(batches)):
         r3_wait(batch)
-    found = rx3[...].reshape(s.no * nq, s.rs, d)
-    sq[0] = jnp.sum(found * found, axis=0)
-    for step in range(1, nh):
-        sq_copy(step).start()
-    for step in range(1, nh):
-        sq_copy(step).wait()
-    sq_ref[...] = jnp.sum(sq[...], axis=0)
-    for q in range(nq):
-        for o in range(s.no):
-            w, at = o * s.rs // m, q * m + o * s.rs % m
-            wg_ref[w, at:at + s.rs, :] = rx3[o, q]
-
+    found_out = pltpu.make_async_copy(rx3, found_hbm, leave.at[0])
+    found_out.start()
+    sq_wait()
+    sq_out = pltpu.make_async_copy(sq.at[pl.ds(0, nh * s.no)], sq_hbm, leave.at[1])
+    sq_out.start()
     for b in range(nb):
         keep_copy(b).wait()
         for step in range(1, nh):
@@ -582,15 +595,21 @@
     for batch, (lo, hi) in enumerate(batches):
         @pl.when(is_owner)
         def _(batch=batch, lo=lo, hi=hi):
-            sent(mine_s.at[pl.ds(0, s.no - 1), lo:hi], r2s.at[batch])
+            sent(rx2.at[pl.ds(0, nh * s.no - 1), lo:hi], r2s.at[batch])
             sent(rx2.at[pl.ds(0, s.naz - 1), lo:hi], r3s.at[batch])
 
         @pl.when(jnp.logical_not(is_owner))
         def _(batch=batch, lo=lo, hi=hi):
-            sent(mine_s.at[:, lo:hi], r2s.at[batch])
-
-
-def finish(blocks, from_hbm, found_ref, sq_ref, out_hbm, wg_ref, held, sem_in, sem_out):
+            sent(rx2.at[pl.ds(0, nh * s.no), lo:hi], r2s.at[batch])
+
+    @pl.when(is_owner)
+    def _():
+        sent(sq.at[pl.ds(0, total - 1)], qs)
+    found_out.wait()
+    sq_out.wait()
+
+
+def finish(s, blocks, from_hbm, found_ref, sq_ref, out_hbm, wg_ref, held, sem_in, sem_out):
     size = held.shape[0] // blocks
 
     def came(b):
@@ -603,9 +622,12 @@
 
     for b in range(blocks):
         came(b).start()
-    squares = jnp.sum(jnp.sum(sq_ref[...], axis=0, keepdims=True), axis=1, keepdims=True)
+    squares = jnp.sum(jnp.sum(sq_ref[...], axis=0), axis=1, keepdims=True)
     factor = jnp.minimum(1.0, CLIP_LIMIT * lax.rsqrt(squares + 1e-06))
-    wg_ref[...] = found_ref[...] * factor
+    for q in range(s.nq):
+        for o in range(s.no):
+            w, at = o * s.rs // s.m, q * s.m + o * s.rs % s.m
+            wg_ref[w, at:at + s.rs, :] = found_ref[o, q] * factor
     for b in range(blocks):
         came(b).wait()
         leaves(b).start()
@@ -618,10 +640,12 @@
     ch = product_grad.shape[1]
     s = Sizes(na, nz, nh, rows, cols, depth, ch)
     vm = pl.BlockSpec(memory_space=pltpu.VMEM)
+    anywhere = pl.BlockSpec(memory_space=pl.ANY)
     dma = pltpu.SemaphoreType.DMA
     half = s.rh // 2
     scratch = [
         pltpu.VMEM((s.rh, cols, depth), BF16),
+        pltpu.VMEM((rows, ch, cols), BF16),
         pltpu.VMEM((ch, rows, cols), BF16),
         pltpu.VMEM((nz, s.cp, s.i, cols), BF16),
         pltpu.VMEM((nh, 4, ch, depth), BF16),
@@ -642,37 +666,35 @@
         pltpu.VMEM((2, s.nc * s.tp, cols), F32),
         pltpu.VMEM((half, depth, 2 * cols), F32),
         pltpu.VMEM((s.rh, cols, depth), BF16),
-        pltpu.VMEM((s.nq, nh, 4 * s.m, depth), F32),
-        pltpu.VMEM((s.nq, nh, 4 * s.m, depth), F32),
+        pltpu.VMEM((s.nq, nh, s.no, s.rs, depth), F32),
+        pltpu.VMEM((s.naz * nh, s.nq, s.rs, depth), F32),
         pltpu.VMEM((s.no, s.nq, s.rs, depth), F32),
-        pltpu.VMEM((s.naz, s.nq, s.rs, depth), F32),
-        pltpu.VMEM((s.no, s.nq, s.rs, depth), F32),
-        pltpu.VMEM((nh, s.rs, depth), F32),
-        dma(()), dma((nh,)), dma((nh,)),
+        pltpu.VMEM((s.naz * nh, 1, depth), F32),
+        dma(()), dma((s.nq,)), dma((nh,)), dma((nh,)),
         dma(()), dma((s.cp, na)), dma((s.nq, 2)), dma((s.cp, nz)),
-        dma(()), dma((s.nq, s.g)), dma((s.nq,)), dma((s.nq, s.nb, s.g)),
+        dma(()), dma((s.nq, s.g)), dma((s.nq,)), dma((s.nq, s.nb + 1, s.g)),
         dma((s.nb, nh)), dma((s.nb, nh)),
-        dma((s.nq, nh)), dma((s.nq, nh)), dma((2,)), dma((2, s.naz)), dma((2,)), dma((2, s.no)),
-        dma((nh,)), dma((nh,)), dma((s.nb,)),
-        dma(()), dma((s.helped,)), dma(()), dma((s.helped, s.nb)),
+        dma((2,)), dma((2, s.naz * nh)), dma((2,)), dma((2, s.no)),
+        dma(()), dma((nh * s.no,)), dma((s.nb,)), dma((2,)),
+        dma(()), dma((s.helped,)), dma(()), dma((s.helped, s.nb + 1)),
     ]
     grad, found, squares = pl.pallas_call(
         functools.partial(kernel, s),
         out_shape=(
             jax.ShapeDtypeStruct((rows, cols, depth), BF16),
-            jax.ShapeDtypeStruct((4, ch, depth), F32),
-            jax.ShapeDtypeStruct((s.rs, depth), F32),
+            jax.ShapeDtypeStruct((s.no, s.nq, s.rs, depth), F32),
+            jax.ShapeDtypeStruct((nh * s.no, 1, depth), F32),
         ),
-        in_specs=[vm, pl.BlockSpec(memory_space=pl.ANY), vm, vm, vm, pl.BlockSpec(memory_space=pltpu.SMEM)],
-        out_specs=(pl.BlockSpec(memory_space=pl.ANY), vm, vm),
+        in_specs=[anywhere, anywhere, vm, vm, vm, pl.BlockSpec(memory_space=pltpu.SMEM)],
+        out_specs=(anywhere, anywhere, anywhere),
         scratch_shapes=scratch,
         compiler_params=pltpu.CompilerParams(
             collective_id=0, has_side_effects=True, vmem_limit_bytes=VMEM_LIMIT),
     )(product_grad, pair_rep, weights.transpose(0, 2, 1), norm_gain.reshape(1, depth),
       residue_mask.reshape(nz, cols), residue_mask)
-    blocks = math.gcd(rows, 8)
+    blocks = math.gcd(rows, 4)
     pair_grad, weight_grads = pl.pallas_call(
-        functools.partial(finish, blocks),
+        functools.partial(finish, s, blocks),
         out_shape=(
             jax.ShapeDtypeStruct((rows, cols, depth), BF16),
             jax.ShapeDtypeStruct((4, ch, depth), F32),

time: 157 us -> 154 us (0.981)
  Pallas kernels: 156 us -> 154 us
    pallas_call x1, Pallas kernels: 151 us -> 149 us  [on_device(): pl.pallas_call(functools.partial(kernel, s), out_shape=(jax.ShapeDtypeStr...]
where the time goes in v5:
time: 154 us
  Pallas kernels  154 us (100%)
    pallas_call x1, Pallas kernels, on_device(): pl.pallas_call(functools.partial(kernel, s), out_shape=(jax.ShapeDtypeStr...  149 us
    pallas_call x1, Pallas kernels, on_device(): pl.pallas_call(functools.partial(finish, s, blocks), out_shape=(jax.Shape...  4.86 us

profile of v5, /device:TPU:0, one launch (start us, length us, event | category | flops | bytes accessed | tf_op | source)
XLA Modules:
  0.0 154.1 jit_solution(14066239143818388397)
XLA Ops:
  0.6 148.6 %shard_map.68 = (bf16[128,128,128]{2,1,0:T(8,128)(2,1)}, f32[8,4,8,128]{3,2,1,0:T(8,128)}, f32[16,1,128]{2,1,0:T(1,128)}) custom-call(bf16[128,64,128]{2,1,0:T(8,128)(2,1)} %p_hbm.1, bf16[128,128,128]{2,1,0:T(8,128)(2,1)} %x_hbm.1, bf16[4,64,128]{2,1,0:T(8,128)(2,1)} %bitcast.4, f32[1,128]{1,0:T(1,128)} %bitcast.6, s32[4,128]{1,0:T(4,128)} %bitcast.5, s32[512]{0:T(512)} %mask_s.1), custom_call_target="tpu_custom_call" | custom-call | tf_op jit(solution)/shard_map/pallas_call | solution.py:681
  149.3 4.9 %shard_map.69 = (bf16[128,128,128]{2,1,0:T(8,128)(2,1)}, f32[4,64,128]{2,1,0:T(8,128)}) custom-call(bf16[128,128,128]{2,1,0:T(8,128)(2,1)} %get-tuple-element.7.from_hbm, f32[8,4,8,128]{3,2,1,0:T(8,128)} %get-tuple-element.8.found_ref, f32[16,1,128]{2,1,0:T(1,128)} %get-tuple-element.9.sq_ref), custom_call_target="tpu_custom_call" | custom-call | tf_op jit(solution)/shard_map/pallas_call | solution.py:696

commit v6 on v5

--- a/solution.py
+++ b/solution.py
@@ -124,11 +124,14 @@
     def pieces(q):
         return [(q * cq + r, 1) for r in range(cq)] if q == 0 else [(q * cq, cq)]
 
+    def spot(c):
+        return c if c < cq else cq - 1 + c // cq
+
     def p_copy(piece, step):
         c, n = piece
         to = lax.rem(a + step, na)
         return send(pt.at[pl.ds((c // cq) * m + to * cq + c % cq, n)], pg.at[z, pl.ds(c, n), pl.ds(a * rb, rb)],
-                    psend, precv.at[c, step], (to, z, h))
+                    psend, precv.at[spot(c)], (to, z, h))
 
     def w_copy(step):
         return send(w_ref, wall.at[h], wsend.at[step], wrecv.at[step], (a, z, lax.rem(h + step, nh)))
@@ -150,7 +153,7 @@
     def z_copy(piece, block, up):
         c, n = piece
         ref = pg.at[block, pl.ds(c, n)]
-        return send(ref, ref, zsend.at[c // cq, 0 if up else 1], zrecv.at[c, block],
+        return send(ref, ref, zsend.at[c // cq, 0 if up else 1], zrecv.at[spot(c), block],
                     (a, z + 1 if up else z - 1, h))
 
     def goes_up(q):
@@ -161,8 +164,7 @@
 
     def z_own(q, some=None):
         for piece in some or pieces(q):
-            for step in range(1, na):
-                p_copy(piece, step).wait_recv()
+            sent(pt.at[pl.ds(0, (na - 1) * piece[1])], precv.at[spot(piece[0])])
 
             @pl.when(goes_up(q))
             def _(piece=piece):
@@ -276,7 +278,7 @@
     def lr_copy(q, step):
         return send(lrs.at[:, pl.ds(q * nc + peer_g(step) * cq, cq)],
                     lrb.at[:, pl.ds(q * cq, cq), pl.ds(row0, rh)],
-                    lsend, lrecv.at[q, step], plane(peer_g(step)))
+                    lsend, lrecv.at[q], plane(peer_g(step)))
 
     for q in [*range(q0, nq), *range(q0)]:
         for step in range(1, g_n):
@@ -307,25 +309,27 @@
         return send(lrb.at[:, pl.ds(q * cq, cq)], lrh.at[:, pl.ds((q - q0) * cq, cq)],
                     hls, hlr.at[q - q0], (a, z_to, h))
 
-    def cuts(q):
-        whole = [(b, 0, cq) for b in range(nb)]
-        if q == nq - 1 and q >= q0 and cq % 2 == 0:
-            return whole[:-1] + [(nb - 1, 0, cq // 2), (nb - 1, cq // 2, cq // 2)]
-        return whole
-
-    def back_copy(q, at, z_to):
-        b, lo, n = cuts(q)[at]
-        return send(gsh.at[:, pl.ds((q - q0) * cq + lo, n), :, pl.ds(b * br, br)],
-                    gs.at[:, pl.ds(q * cq + lo, n), :, pl.ds(b * br, br)],
-                    hgs, hgr.at[q - q0, at], (a, z_to, h))
-
-    def g_copy(q, at, step):
-        b, lo, n = cuts(q)[at]
+    def g_copy(q, b, step):
         g = peer_g(step)
         place = lax.rem(g, na) * nh + lax.div(g, na)
-        return send(gs.at[:, pl.ds(q * cq + lo, n), place, pl.ds(b * br, br)],
-                    gr.at[:, pl.ds(q * nc + me_g * cq + lo, n), pl.ds(b * br, br)],
-                    gsend.at[q], grecv.at[q, at, step], plane(g))
+        return send(gs.at[:, pl.ds(q * cq, cq), place, pl.ds(b * br, br)],
+                    gr.at[:, pl.ds(q * nc + me_g * cq, cq), pl.ds(b * br, br)],
+                    gsend.at[q], grecv.at[q, b], plane(g))
+
+    def back_copy(q, b, z_to):
+        return send(gsh.at[:, pl.ds((q - q0) * cq, cq), :, pl.ds(b * br, br)],
+                    gs.at[:, pl.ds(q * cq, cq), :, pl.ds(b * br, br)],
+                    hgs, hgr.at[q - q0, b], (a, z_to, h))
+
+    def direct(q):
+        return q == nq - 1 and q >= q0
+
+    def direct_copy(q, b, step):
+        g = peer_g(step)
+        place = lax.rem(g, na) * nh + lax.div(g, na)
+        return send(gsh.at[:, pl.ds((q - q0) * cq, cq), place, pl.ds(b * br, br)],
+                    gr.at[:, pl.ds(q * nc + me_g * cq, cq), pl.ds(b * br, br)],
+                    hgs, grecv.at[q, b], (lax.rem(g, na), outward, lax.div(g, na)))
 
     def out_copy(b, step):
         return send(outv.at[pl.ds(b * br, br)], out_hbm.at[pl.ds(h * rh + b * br, br)],
@@ -353,7 +357,7 @@
     def r2_copy(batch, half, o, sender):
         lo, hi = batches[batch]
         return send(raw.at[lo:hi, half, o], rx2.at[sender, lo:hi],
-                    r2s.at[batch], r2r.at[batch, sender], (*owner(o), half))
+                    r2s.at[batch], r2r.at[batch], (*owner(o), half))
 
     def r2_start(batch):
         for half in range(nh):
@@ -365,11 +369,11 @@
     def r3_copy(batch, o, step):
         lo, hi = batches[batch]
         ref = rx3.at[o, lo:hi]
-        return send(ref, ref, r3s.at[batch], r3r.at[batch, o], at_n(lax.rem(me_n + step, s.naz)))
+        return send(ref, ref, r3s.at[batch], r3r.at[batch], at_n(lax.rem(me_n + step, s.naz)))
 
     def sq_copy(slot, step):
         ref = sq.at[slot]
-        return send(ref, ref, qs, qr.at[slot], at_t(lax.rem(me_t + step, total)))
+        return send(ref, ref, qs, qr, at_t(lax.rem(me_t + step, total)))
 
     def r2_sum(batch):
         lo, hi = batches[batch]
@@ -377,9 +381,8 @@
         @pl.when(is_owner)
         def _():
             def one(step, mine):
-                n = lax.rem(me_t + step, total)
-                r2_copy(batch, 0, 0, n).wait_recv()
-                return mine + rx2[n, lo:hi]
+                return mine + rx2[lax.rem(me_t + step, total), lo:hi]
+            sent(rx2.at[pl.ds(0, total - 1), lo:hi], r2r.at[batch])
             rx3[me_o, lo:hi] = lax.fori_loop(1, total, one, raw[lo:hi, h, me_o])
             for step in range(1, s.naz):
                 r3_copy(batch, me_o, step).start()
@@ -390,23 +393,36 @@
                 for step in range(1, total):
                     sq_copy(slot, step).start()
 
+    def at_role(wait):
+        @pl.when(is_owner)
+        def _():
+            wait(1)
+
+        @pl.when(jnp.logical_not(is_owner))
+        def _():
+            wait(0)
+
     def r3_wait(batch):
-        for o in range(s.no):
-            @pl.when(other(o))
-            def _(o=o):
-                r3_copy(batch, o, 1).wait_recv()
+        lo, hi = batches[batch]
+        at_role(lambda own: sent(rx2.at[pl.ds(0, s.no - own), lo:hi], r3r.at[batch]))
 
     def sq_wait():
-        for half in range(nh):
-            for o in range(s.no):
-                @pl.when(other(o, half))
-                def _(slot=half * s.no + o):
-                    sq_copy(slot, 1).wait_recv()
+        at_role(lambda own: sent(sq.at[pl.ds(0, nh * s.no - own)], qr))
 
     def gather(q, b):
-        for at, cut in enumerate(cuts(q)):
-            for step in range(1, g_n if cut[0] == b else 1):
-                g_copy(q, at, step).wait_recv()
+        def came(count):
+            sent(gr.at[:, pl.ds(0, count * cq), pl.ds(0, br)], grecv.at[q, b])
+
+        if direct(q):
+            @pl.when(is_end)
+            def _():
+                came(g_n)
+
+            @pl.when(jnp.logical_not(is_end))
+            def _():
+                came(g_n - 1)
+        else:
+            came(g_n - 1)
 
         def spread(n, carry):
             for side in range(2):
@@ -454,17 +470,23 @@
             out_copy(b, step).start()
 
     def lr_wait(q):
+        sent(lrs.at[:, pl.ds(0, (g_n - 1) * cq)], lrecv.at[q])
+
+    def g_out(q, b):
         for step in range(1, g_n):
-            lr_copy(q, step).wait_recv()
-
-    def g_send(q, at):
-        b, lo, n = cuts(q)[at]
-        for step in range(1, g_n):
-            g_copy(q, at, step).start()
+            g_copy(q, b, step).start()
         for side in range(2):
-            for r in range(lo, lo + n):
+            for r in range(cq):
                 gr[side, q * nc + me_g * cq + r, b * br:(b + 1) * br, :] = gs[
                     side, q * cq + r, a * nh + h, b * br:(b + 1) * br, :]
+
+    def g_send(q, b):
+        if direct(q):
+            @pl.when(jnp.logical_not(is_end))
+            def _():
+                g_out(q, b)
+        else:
+            g_out(q, b)
 
     def make(q):
         if q < q0:
@@ -478,8 +500,12 @@
             z_rest(q)
             in_copy(q, outward).wait_recv()
             triangles(q, lrh, gsh, q0)
-            for at in range(len(cuts(q))):
-                back_copy(q, at, outward).start()
+            for b in range(nb):
+                if direct(q):
+                    for step in range(g_n):
+                        direct_copy(q, b, step).start()
+                else:
+                    back_copy(q, b, outward).start()
             lr_wait(q)
             triangles(q, lrb, gs, 0)
 
@@ -489,11 +515,11 @@
             lr_wait(q)
             triangles(q, lrb, gs, 0)
 
-    def came_back(q, at):
-        if q >= q0:
+    def came_back(q, b):
+        if q >= q0 and not direct(q):
             @pl.when(is_end)
             def _():
-                back_copy(q, at, outward).wait_recv()
+                back_copy(q, b, outward).wait_recv()
 
     for hop in range(1, nz - 1):
         for q in range(q0):
@@ -522,7 +548,12 @@
         sent(pt.at[pl.ds(0, (na - 1) * s.cp)], psend)
         sent(lrs.at[:, pl.ds(0, (g_n - 1) * nq * cq)], lsend)
         for q in range(nq):
-            sent(gs.at[:, pl.ds(q * cq, cq), pl.ds(0, g_n - 1)], gsend.at[q])
+            if direct(q):
+                @pl.when(jnp.logical_not(is_end))
+                def _(q=q):
+                    sent(gs.at[:, pl.ds(q * cq, cq), pl.ds(0, g_n - 1)], gsend.at[q])
+            else:
+                sent(gs.at[:, pl.ds(q * cq, cq), pl.ds(0, g_n - 1)], gsend.at[q])
             for count in range(1, nz):
                 @pl.when((z + 1 == count) & goes_up(q))
                 def _(q=q, count=count):
@@ -559,14 +590,13 @@
         if q == last:
             queue += [(last - 1, b) for b in range(nb)] if q else []
             run(max(len(queue) - 2 * nb, 0))
-        ways = cuts(q)
-        for at, (b, lo, n) in enumerate(ways):
+        for b in range(nb):
             run(1 if q < last else 0)
-            came_back(q, at)
-            g_send(q, at)
+            came_back(q, b)
+            g_send(q, b)
             if q == last:
-                run(3 if b < nb - 1 else 1 if at < len(ways) - 1 else 0)
-                if b and not lo:
+                run(3 if b < nb - 1 else 0)
+                if b:
                     queue.append((last, b - 1))
     queue.append((last, nb - 1))
     run(max(len(queue) - 1, 0))
@@ -671,12 +701,12 @@
         pltpu.VMEM((s.no, s.nq, s.rs, depth), F32),
         pltpu.VMEM((s.naz * nh, 1, depth), F32),
         dma(()), dma((s.nq,)), dma((nh,)), dma((nh,)),
-        dma(()), dma((s.cp, na)), dma((s.nq, 2)), dma((s.cp, nz)),
-        dma(()), dma((s.nq, s.g)), dma((s.nq,)), dma((s.nq, s.nb + 1, s.g)),
+        dma(()), dma((s.cq + s.nq,)), dma((s.nq, 2)), dma((s.cq + s.nq, nz)),
+        dma(()), dma((s.nq,)), dma((s.nq,)), dma((s.nq, s.nb)),
         dma((s.nb, nh)), dma((s.nb, nh)),
-        dma((2,)), dma((2, s.naz * nh)), dma((2,)), dma((2, s.no)),
-        dma(()), dma((nh * s.no,)), dma((s.nb,)), dma((2,)),
-        dma(()), dma((s.helped,)), dma(()), dma((s.helped, s.nb + 1)),
+        dma((2,)), dma((2,)), dma((2,)), dma((2,)),
+        dma(()), dma(()), dma((s.nb,)), dma((2,)),
+        dma(()), dma((s.helped,)), dma(()), dma((s.helped, s.nb)),
     ]
     grad, found, squares = pl.pallas_call(
         functools.partial(kernel, s),

time: 154 us -> 149 us (0.968)
  Pallas kernels: 154 us -> 148 us
    pallas_call x1, Pallas kernels: 149 us -> 143 us  [on_device(): pl.pallas_call(functools.partial(kernel, s), out_shape=(jax.ShapeDtypeStr...]
where the time goes in v6:
time: 149 us
  Pallas kernels  148 us (99%)
    pallas_call x1, Pallas kernels, on_device(): pl.pallas_call(functools.partial(kernel, s), out_shape=(jax.ShapeDtypeStr...  143 us
    pallas_call x1, Pallas kernels, on_device(): pl.pallas_call(functools.partial(finish, s, blocks), out_shape=(jax.Shape...  4.86 us

profile of v6, /device:TPU:0, one launch (start us, length us, event | category | flops | bytes accessed | tf_op | source)
XLA Modules:
  0.0 148.9 jit_solution(2516028708081494299)
XLA Ops:
  0.6 143.4 %shard_map.68 = (bf16[128,128,128]{2,1,0:T(8,128)(2,1)}, f32[8,4,8,128]{3,2,1,0:T(8,128)}, f32[16,1,128]{2,1,0:T(1,128)}) custom-call(bf16[128,64,128]{2,1,0:T(8,128)(2,1)} %p_hbm.1, bf16[128,128,128]{2,1,0:T(8,128)(2,1)} %x_hbm.1, bf16[4,64,128]{2,1,0:T(8,128)(2,1)} %bitcast.4, f32[1,128]{1,0:T(1,128)} %bitcast.6, s32[4,128]{1,0:T(4,128)} %bitcast.5, s32[512]{0:T(512)} %mask_s.1), custom_call_target="tpu_custom_call" | custom-call | tf_op jit(solution)/shard_map/pallas_call | solution.py:711
  144.0 4.9 %shard_map.69 = (bf16[128,128,128]{2,1,0:T(8,128)(2,1)}, f32[4,64,128]{2,1,0:T(8,128)}) custom-call(bf16[128,128,128]{2,1,0:T(8,128)(2,1)} %get-tuple-element.7.from_hbm, f32[8,4,8,128]{3,2,1,0:T(8,128)} %get-tuple-element.8.found_ref, f32[16,1,128]{2,1,0:T(1,128)} %get-tuple-element.9.sq_ref), custom_call_target="tpu_custom_call" | custom-call | tf_op jit(solution)/shard_map/pallas_call | solution.py:726

commit v7 on v6

--- a/solution.py
+++ b/solution.py
@@ -270,10 +270,10 @@
     for q in range(nb, q0):
         z_own(q)
 
-    @pl.when(is_end)
-    def _():
-        for q in range(q0, nq):
-            z_own(q)
+    if q0 < nq:
+        @pl.when(is_end)
+        def _():
+            z_own(q0)
 
     def lr_copy(q, step):
         return send(lrs.at[:, pl.ds(q * nc + peer_g(step) * cq, cq)],
@@ -488,13 +488,7 @@
         else:
             g_out(q, b)
 
-    def make(q):
-        if q < q0:
-            z_rest(q)
-            lr_wait(q)
-            triangles(q, lrb, gs, 0)
-            return
-
+    def help_end(q):
         @pl.when(is_near)
         def _():
             z_rest(q)
@@ -506,12 +500,20 @@
                         direct_copy(q, b, step).start()
                 else:
                     back_copy(q, b, outward).start()
+
+    def make(q):
+        if q < q0:
+            z_rest(q)
             lr_wait(q)
             triangles(q, lrb, gs, 0)
+            return
 
         @pl.when(jnp.logical_not(is_near | is_end))
         def _():
             z_rest(q)
+
+        @pl.when(jnp.logical_not(is_end))
+        def _():
             lr_wait(q)
             triangles(q, lrb, gs, 0)
 
@@ -541,6 +543,8 @@
         for q in range(q0, nq):
             lr_wait(q)
             in_copy(q, inward).start()
+            if q + 1 < nq:
+                z_own(q + 1)
 
     def drain():
         for step in range(1, nh):
@@ -584,6 +588,10 @@
                 r2_start(final)
 
     for q in range(nq):
+        if q == q0 - 1 and q0 < nq:
+            help_end(q0)
+        elif q > q0:
+            help_end(q)
         make(q)
         if q > 1:
             queue += [(q - 2, b) for b in range(nb)]

time: 149 us -> 151 us (1.013)
  Pallas kernels: 148 us -> 150 us
where the time goes in v7:
time: 151 us; the launch traced here: 150 us
  Pallas kernels  150 us (99%)
    pallas_call x1, Pallas kernels, on_device(): pl.pallas_call(functools.partial(kernel, s), out_shape=(jax.ShapeDtypeStr...  145 us
    pallas_call x1, Pallas kernels, on_device(): pl.pallas_call(functools.partial(finish, s, blocks), out_shape=(jax.Shape...  4.86 us

profile of v7, /device:TPU:0, one launch (start us, length us, event | category | flops | bytes accessed | tf_op | source)
XLA Modules:
  0.0 150.3 jit_solution(2877172373848387953)
XLA Ops:
  0.6 144.8 %shard_map.68 = (bf16[128,128,128]{2,1,0:T(8,128)(2,1)}, f32[8,4,8,128]{3,2,1,0:T(8,128)}, f32[16,1,128]{2,1,0:T(1,128)}) custom-call(bf16[128,64,128]{2,1,0:T(8,128)(2,1)} %p_hbm.1, bf16[128,128,128]{2,1,0:T(8,128)(2,1)} %x_hbm.1, bf16[4,64,128]{2,1,0:T(8,128)(2,1)} %bitcast.4, f32[1,128]{1,0:T(1,128)} %bitcast.6, s32[4,128]{1,0:T(4,128)} %bitcast.5, s32[512]{0:T(512)} %mask_s.1), custom_call_target="tpu_custom_call" | custom-call | tf_op jit(solution)/shard_map/pallas_call | solution.py:719
  145.5 4.9 %shard_map.69 = (bf16[128,128,128]{2,1,0:T(8,128)(2,1)}, f32[4,64,128]{2,1,0:T(8,128)}) custom-call(bf16[128,128,128]{2,1,0:T(8,128)(2,1)} %get-tuple-element.7.from_hbm, f32[8,4,8,128]{3,2,1,0:T(8,128)} %get-tuple-element.8.found_ref, f32[16,1,128]{2,1,0:T(1,128)} %get-tuple-element.9.sq_ref), custom_call_target="tpu_custom_call" | custom-call | tf_op jit(solution)/shard_map/pallas_call | solution.py:734

commit v8 on v7

--- a/solution.py
+++ b/solution.py
@@ -530,13 +530,17 @@
             @pl.when(jnp.logical_not(is_end))
             def _():
                 z_own(q0)
-    for q in range(q0, nq):
+    def relay_on(q):
+        if q >= nq:
+            return
         for hop in range(1, nz - 1):
             z_forward(q, hop)
         if q + 1 < nq:
             @pl.when(jnp.logical_not(is_end))
-            def _(q=q):
+            def _():
                 z_own(q + 1)
+
+    relay_on(q0)
 
     @pl.when(is_end)
     def _():
@@ -590,8 +594,10 @@
     for q in range(nq):
         if q == q0 - 1 and q0 < nq:
             help_end(q0)
+            relay_on(q0 + 1)
         elif q > q0:
             help_end(q)
+            relay_on(q + 1)
         make(q)
         if q > 1:
             queue += [(q - 2, b) for b in range(nb)]

time: 151 us -> 147 us (0.974)
  Pallas kernels: 150 us -> 146 us
    pallas_call x1, Pallas kernels: 145 us -> 142 us  [on_device(): pl.pallas_call(functools.partial(kernel, s), out_shape=(jax.ShapeDtypeStr...]
where the time goes in v8:
time: 147 us
  Pallas kernels  146 us (99%)
    pallas_call x1, Pallas kernels, on_device(): pl.pallas_call(functools.partial(kernel, s), out_shape=(jax.ShapeDtypeStr...  142 us
    pallas_call x1, Pallas kernels, on_device(): pl.pallas_call(functools.partial(finish, s, blocks), out_shape=(jax.Shape...  4.86 us

profile of v8, /device:TPU:0, one launch (start us, length us, event | category | flops | bytes accessed | tf_op | source)
XLA Modules:
  0.0 147.0 jit_solution(15779945155773534008)
XLA Ops:
  0.6 141.5 %shard_map.68 = (bf16[128,128,128]{2,1,0:T(8,128)(2,1)}, f32[8,4,8,128]{3,2,1,0:T(8,128)}, f32[16,1,128]{2,1,0:T(1,128)}) custom-call(bf16[128,64,128]{2,1,0:T(8,128)(2,1)} %p_hbm.1, bf16[128,128,128]{2,1,0:T(8,128)(2,1)} %x_hbm.1, bf16[4,64,128]{2,1,0:T(8,128)(2,1)} %bitcast.4, f32[1,128]{1,0:T(1,128)} %bitcast.6, s32[4,128]{1,0:T(4,128)} %bitcast.5, s32[512]{0:T(512)} %mask_s.1), custom_call_target="tpu_custom_call" | custom-call | tf_op jit(solution)/shard_map/pallas_call | solution.py:725
  142.2 4.9 %shard_map.69 = (bf16[128,128,128]{2,1,0:T(8,128)(2,1)}, f32[4,64,128]{2,1,0:T(8,128)}) custom-call(bf16[128,128,128]{2,1,0:T(8,128)(2,1)} %get-tuple-element.7.from_hbm, f32[8,4,8,128]{3,2,1,0:T(8,128)} %get-tuple-element.8.found_ref, f32[16,1,128]{2,1,0:T(1,128)} %get-tuple-element.9.sq_ref), custom_call_target="tpu_custom_call" | custom-call | tf_op jit(solution)/shard_map/pallas_call | solution.py:740

commit v9 on v8

--- a/solution.py
+++ b/solution.py
@@ -122,10 +122,12 @@
         lax.fori_loop(0, rb // s.bi, block, 0)
 
     def pieces(q):
-        return [(q * cq + r, 1) for r in range(cq)] if q == 0 else [(q * cq, cq)]
+        return [(q * cq + r, 1) for r in range(cq)] if q in (0, q0) else [(q * cq, cq)]
+
+    starts = [piece[0] for q in range(nq) for piece in pieces(q)]
 
     def spot(c):
-        return c if c < cq else cq - 1 + c // cq
+        return starts.index(c)
 
     def p_copy(piece, step):
         c, n = piece
@@ -187,18 +189,18 @@
                 z_copy(piece, z + hop, False).wait_recv()
                 z_copy(piece, z + hop, False).start()
 
-    def z_rest(q):
+    def z_rest(q, some=None):
         for hop in range(1, nz):
             here = True if q < q0 else jnp.logical_not(is_end)
 
             @pl.when((z >= hop) & jnp.logical_not(goes_up(q)) & here)
             def _(hop=hop):
-                for piece in pieces(q):
+                for piece in some or pieces(q):
                     z_copy(piece, z - hop, True).wait_recv()
 
             @pl.when((z + hop < nz) & jnp.logical_not(goes_down(q)) & here)
             def _(hop=hop):
-                for piece in pieces(q):
+                for piece in some or pieces(q):
                     z_copy(piece, z + hop, False).wait_recv()
 
     eye_d = eye(d)
@@ -305,9 +307,9 @@
             return carry
         lax.fori_loop(0, cq, one, 0)
 
-    def in_copy(q, z_to):
-        return send(lrb.at[:, pl.ds(q * cq, cq)], lrh.at[:, pl.ds((q - q0) * cq, cq)],
-                    hls, hlr.at[q - q0], (a, z_to, h))
+    def in_copy(q, r, z_to):
+        at = (q - q0) * cq + r
+        return send(lrb.at[:, pl.ds(q * cq + r, 1)], lrh.at[:, pl.ds(at, 1)], hls, hlr.at[at], (a, z_to, h))
 
     def g_copy(q, b, step):
         g = peer_g(step)
@@ -491,9 +493,13 @@
     def help_end(q):
         @pl.when(is_near)
         def _():
-            z_rest(q)
-            in_copy(q, outward).wait_recv()
-            triangles(q, lrh, gsh, q0)
+            if q != q0:
+                z_rest(q)
+            for r in range(cq):
+                if q == q0:
+                    z_rest(q, [pieces(q)[r]])
+                in_copy(q, r, outward).wait_recv()
+                triangle(q * cq + r, lrh, (q - q0) * cq + r, gsh)
             for b in range(nb):
                 if direct(q):
                     for step in range(g_n):
@@ -546,7 +552,8 @@
     def _():
         for q in range(q0, nq):
             lr_wait(q)
-            in_copy(q, inward).start()
+            for r in range(cq):
+                in_copy(q, r, inward).start()
             if q + 1 < nq:
                 z_own(q + 1)
 
@@ -715,12 +722,12 @@
         pltpu.VMEM((s.no, s.nq, s.rs, depth), F32),
         pltpu.VMEM((s.naz * nh, 1, depth), F32),
         dma(()), dma((s.nq,)), dma((nh,)), dma((nh,)),
-        dma(()), dma((s.cq + s.nq,)), dma((s.nq, 2)), dma((s.cq + s.nq, nz)),
+        dma(()), dma((2 * s.cq + s.nq,)), dma((s.nq, 2)), dma((2 * s.cq + s.nq, nz)),
         dma(()), dma((s.nq,)), dma((s.nq,)), dma((s.nq, s.nb)),
         dma((s.nb, nh)), dma((s.nb, nh)),
         dma((2,)), dma((2,)), dma((2,)), dma((2,)),
         dma(()), dma(()), dma((s.nb,)), dma((2,)),
-        dma(()), dma((s.helped,)), dma(()), dma((s.helped, s.nb)),
+        dma(()), dma((s.helped * s.cq,)), dma(()), dma((s.helped, s.nb)),
     ]
     grad, found, squares = pl.pallas_call(
         functools.partial(kernel, s),

time: 147 us -> 146 us (level)
  no operation moved by 1% of the time
where the time goes in v9:
time: 146 us
  Pallas kernels  145 us (99%)
    pallas_call x1, Pallas kernels, on_device(): pl.pallas_call(functools.partial(kernel, s), out_shape=(jax.ShapeDtypeStr...  140 us
    pallas_call x1, Pallas kernels, on_device(): pl.pallas_call(functools.partial(finish, s, blocks), out_shape=(jax.Shape...  4.86 us

profile of v9, /device:TPU:0, one launch (start us, length us, event | category | flops | bytes accessed | tf_op | source)
XLA Modules:
  0.0 145.6 jit_solution(7677276853952429623)
XLA Ops:
  0.6 140.1 %shard_map.68 = (bf16[128,128,128]{2,1,0:T(8,128)(2,1)}, f32[8,4,8,128]{3,2,1,0:T(8,128)}, f32[16,1,128]{2,1,0:T(1,128)}) custom-call(bf16[128,64,128]{2,1,0:T(8,128)(2,1)} %p_hbm.1, bf16[128,128,128]{2,1,0:T(8,128)(2,1)} %x_hbm.1, bf16[4,64,128]{2,1,0:T(8,128)(2,1)} %bitcast.4, f32[1,128]{1,0:T(1,128)} %bitcast.6, s32[4,128]{1,0:T(4,128)} %bitcast.5, s32[512]{0:T(512)} %mask_s.1), custom_call_target="tpu_custom_call" | custom-call | tf_op jit(solution)/shard_map/pallas_call | solution.py:732
  140.7 4.9 %shard_map.69 = (bf16[128,128,128]{2,1,0:T(8,128)(2,1)}, f32[4,64,128]{2,1,0:T(8,128)}) custom-call(bf16[128,128,128]{2,1,0:T(8,128)(2,1)} %get-tuple-element.7.from_hbm, f32[8,4,8,128]{3,2,1,0:T(8,128)} %get-tuple-element.8.found_ref, f32[16,1,128]{2,1,0:T(1,128)} %get-tuple-element.9.sq_ref), custom_call_target="tpu_custom_call" | custom-call | tf_op jit(solution)/shard_map/pallas_call | solution.py:747

commit v10 on v9

--- a/solution.py
+++ b/solution.py
@@ -10,7 +10,7 @@
 
 CLIP_LIMIT = 64.0
 MAX_CHUNKS = 4
-ROWS_AT_ONCE = 2
+ROWS_AT_ONCE = 4
 VMEM_LIMIT = 66 * 1000 * 1000
 MESH = pl.DeviceIdType.MESH
 NT = (((1,), (1,)), ((), ()))

time: 146 us -> 146 us (level)
  no operation moved by 1% of the time
where the time goes in v10:
time: 146 us; the launch traced here: 145 us
  Pallas kernels  145 us (99%)
    pallas_call x1, Pallas kernels, on_device(): pl.pallas_call(functools.partial(kernel, s), out_shape=(jax.ShapeDtypeStr...  140 us
    pallas_call x1, Pallas kernels, on_device(): pl.pallas_call(functools.partial(finish, s, blocks), out_shape=(jax.Shape...  4.86 us

profile of v10, /device:TPU:0, one launch (start us, length us, event | category | flops | bytes accessed | tf_op | source)
XLA Modules:
  0.0 145.4 jit_solution(17441290938240754736)
XLA Ops:
  0.6 139.8 %shard_map.68 = (bf16[128,128,128]{2,1,0:T(8,128)(2,1)}, f32[8,4,8,128]{3,2,1,0:T(8,128)}, f32[16,1,128]{2,1,0:T(1,128)}) custom-call(bf16[128,64,128]{2,1,0:T(8,128)(2,1)} %p_hbm.1, bf16[128,128,128]{2,1,0:T(8,128)(2,1)} %x_hbm.1, bf16[4,64,128]{2,1,0:T(8,128)(2,1)} %bitcast.4, f32[1,128]{1,0:T(1,128)} %bitcast.6, s32[4,128]{1,0:T(4,128)} %bitcast.5, s32[512]{0:T(512)} %mask_s.1), custom_call_target="tpu_custom_call" | custom-call | tf_op jit(solution)/shard_map/pallas_call | solution.py:732
  140.4 4.9 %shard_map.69 = (bf16[128,128,128]{2,1,0:T(8,128)(2,1)}, f32[4,64,128]{2,1,0:T(8,128)}) custom-call(bf16[128,128,128]{2,1,0:T(8,128)(2,1)} %get-tuple-element.7.from_hbm, f32[8,4,8,128]{3,2,1,0:T(8,128)} %get-tuple-element.8.found_ref, f32[16,1,128]{2,1,0:T(1,128)} %get-tuple-element.9.sq_ref), custom_call_target="tpu_custom_call" | custom-call | tf_op jit(solution)/shard_map/pallas_call | solution.py:747
